TPU v7x, 32 devices: a whole 2x2x4 slice. The times are simulated.
32 devices in a mesh: dp: 4 (over z), expert: 8 (over y, x, core).
Axes of the slice: x: 2, y: 2, z: 4, core: 2. Of those that a mesh axis runs over, the one named last changes fastest.
Arguments:
- tokens: bfloat16 [32, 212, 1024], P(('dp', 'expert')), may hold values from -6 to 6
- expert_ids: int32 [32, 212, 1], P(('dp', 'expert')), may hold values from 0 to 7; in each aligned block of 212 rows (0 to 211, 212 to 423, ..., all dimensions but the last counted through in order) at most 36 rows name the same one
- caption_lengths: int32 [32], P(('dp', 'expert')), may hold values from 1 to 16, as said below
- layer_norm_gain: float32 [1024], replicated, may hold values from 0.5 to 1.5
- router: float32 [1024, 8], replicated, may hold values from -0.1875 to 0.1875
- w_up: bfloat16 [8, 1024, 4096], P('expert', None, 'dp'), may hold values from -0.1875 to 0.1875
- w_down: bfloat16 [8, 4096, 1024], P('expert', 'dp'), may hold values from -0.09375 to 0.09375
- logit_scale: float32 [1], replicated, may hold values from 5 to 20
- logit_bias: float32 [1], replicated, may hold values from -4 to -1.5
Outputs:
- loss: float32 [1], replicated
- grad_tokens: bfloat16 [32, 212, 1024], P(('dp', 'expert'))
- grad_up: float32 [8, 1024, 4096], P('expert', None, 'dp')
- grad_down: float32 [8, 4096, 1024], P('expert', 'dp')
- grad_router: float32 [1024, 8], replicated
- layer_gain_gradient: float32 [1024], replicated
Inputs may be any that keep to these rules, and one draw needn't show every extreme that they name: `expert_ids`: among the rows of one device (aligned blocks of 212 rows, devices ordered by dp then expert) no expert is named more than 36 times, a bound that some block reaches. `caption_lengths`: some caption has all 16 tokens.
All inputs are finite; a program needn't handle non-finite values.
Results may differ from a plain program's by a relative error of at most 0.009.
Values may be sent and summed in bfloat16 or wider, within the bound.
A program may use at most 128 MiB of HBM per device.

v0:
```python
import jax
import jax.numpy as jnp
from jax import lax
from jax.sharding import PartitionSpec as P

D = 1024
PATCH = 196
CAPLEN = 16
SEQ = 212


eps = 1e-06
loss_scale = 1024.0


def gelu_slope(pre):
    return (
        0.5 * (1.0 + lax.erf(pre * 0.7071067811865476))
        + pre * jnp.exp(-0.5 * pre * pre) * 0.3989422804014327
    )


def deliver(buffer, experts, slots):
    width = buffer.shape[-1]
    sent = lax.all_to_all(
        buffer.reshape(experts, 1, slots, width), "expert", split_axis=0, concat_axis=1, tiled=True
    )
    shaped = sent.reshape(sent.shape[0], 1, sent.shape[1], slots, width)
    whole = lax.all_gather(shaped, "dp", axis=1, tiled=True)
    return whole.reshape(whole.shape[0], -1, width)


def give_back(partial_value, n_dp, n_expert, slots):
    local = partial_value.shape[0]
    width = partial_value.shape[-1]
    summed = lax.psum_scatter(
        partial_value.reshape(local, n_dp, n_expert * slots, width).astype(jnp.bfloat16),
        "dp",
        scatter_dimension=1,
        tiled=True,
    )
    rounded = summed.reshape(local, n_expert, slots, width)
    returned = lax.all_to_all(rounded, "expert", split_axis=1, concat_axis=0, tiled=True)
    return returned.reshape(-1, width)


def body(
    tokens,
    expert_ids,
    caption_lengths,
    layer_norm_gain,
    router,
    w_up,
    w_down,
    logit_scale,
    logit_bias,
):
    n_dp = lax.axis_size("dp")
    n_expert = lax.axis_size("expert")
    pair_dev = tokens.shape[0]
    rows = pair_dev * SEQ
    experts = router.shape[1]
    slots = rows * 4 // (3 * experts) + 1
    pairs_all = pair_dev * n_dp * n_expert
    input_rows = tokens.reshape(rows, D).astype(jnp.float32)
    input_mean = jnp.mean(input_rows, axis=1, keepdims=True)
    var_x = jnp.mean((input_rows - input_mean) ** 2, axis=1, keepdims=True)
    inverse_deviation = 1.0 / jnp.sqrt(var_x + eps)
    centered_scaled_input = (input_rows - input_mean) * inverse_deviation
    normalized_input = (centered_scaled_input * layer_norm_gain).astype(jnp.bfloat16)
    ids = expert_ids.reshape(rows)
    onehot = (ids[:, None] == jnp.arange(experts, dtype=jnp.int32)[None, :]).astype(jnp.int32)
    slot = jnp.sum((jnp.cumsum(onehot, axis=0) - 1) * onehot, axis=1)
    dest = ids * slots + slot
    onehot_f = onehot.astype(jnp.float32)
    buffer = jnp.zeros((experts * slots, D), jnp.bfloat16).at[dest].set(normalized_input)
    gathered = deliver(buffer, experts, slots)
    pre = jnp.einsum("erd,edf->erf", gathered, w_up, preferred_element_type=jnp.float32)
    act = jax.nn.gelu(pre, approximate=False).astype(jnp.bfloat16)
    partial_value = jnp.einsum("erf,efd->erd", act, w_down, preferred_element_type=jnp.float32)
    moe = give_back(partial_value, n_dp, n_expert, slots)[dest].astype(jnp.float32)
    xnf = normalized_input.astype(jnp.float32)
    router_logits = jnp.dot(xnf, router, precision=lax.Precision.HIGHEST)
    gate = jax.nn.sigmoid(jnp.sum(router_logits * onehot_f, axis=1))
    y = (input_rows + gate[:, None] * moe).reshape(pair_dev, SEQ, D)
    img = jnp.mean(y[:, :PATCH], axis=1)
    lengths = caption_lengths.astype(jnp.float32)
    mask = (jnp.arange(CAPLEN, dtype=jnp.int32)[None, :] < caption_lengths[:, None]).astype(
        jnp.float32
    )
    txt = jnp.sum(y[:, PATCH:] * mask[:, :, None], axis=1) / lengths[:, None]
    ru = jnp.sqrt(jnp.mean(img * img, axis=1, keepdims=True) + eps)
    rv = jnp.sqrt(jnp.mean(txt * txt, axis=1, keepdims=True) + eps)
    u = img / ru
    v = txt / rv
    scale = logit_scale[0]
    first = lax.axis_index(("dp", "expert")) * pair_dev
    mine = first + jnp.arange(pair_dev, dtype=jnp.int32)
    every = jnp.arange(pairs_all, dtype=jnp.int32)
    own_sign = jnp.where(mine[:, None] == every[None, :], 1.0, -1.0)
    u_all, v_all = (
        lax.all_gather(u, ("dp", "expert"), axis=0, tiled=True),
        lax.all_gather(v, ("dp", "expert"), axis=0, tiled=True),
    )
    logits = scale * jnp.dot(u, v_all.T, precision=lax.Precision.HIGHEST) / D + logit_bias[0]
    loss_term = -jnp.sum(jax.nn.log_sigmoid(own_sign * logits)) / pairs_all
    coef = -(loss_scale / pairs_all) * own_sign * jax.nn.sigmoid(-own_sign * logits)
    du = scale / D * jnp.dot(coef, v_all, precision=lax.Precision.HIGHEST)
    column_logits = scale * jnp.dot(u_all, v.T, precision=lax.Precision.HIGHEST) / D + logit_bias[0]
    column_sign = own_sign.T
    column_coef = (
        -(loss_scale / pairs_all) * column_sign * jax.nn.sigmoid(-column_sign * column_logits)
    )
    dv = scale / D * jnp.dot(column_coef.T, u_all, precision=lax.Precision.HIGHEST)
    dimg = (du - u * jnp.mean(du * u, axis=1, keepdims=True)) / ru
    dtxt = (dv - v * jnp.mean(dv * v, axis=1, keepdims=True)) / rv
    dy_img = jnp.broadcast_to(dimg[:, None, :] / PATCH, (pair_dev, PATCH, D))
    dy_txt = (dtxt / lengths[:, None])[:, None, :] * mask[:, :, None]
    dy = jnp.concatenate([dy_img, dy_txt], axis=1).reshape(rows, D)
    dmoe = (gate[:, None] * dy).astype(jnp.bfloat16)
    dgl = jnp.sum(dy * moe, axis=1) * gate * (1.0 - gate)
    router_part = jnp.dot(xnf.T, onehot_f * dgl[:, None], precision=lax.Precision.HIGHEST)
    grad_buffer = jnp.zeros((experts * slots, D), jnp.bfloat16).at[dest].set(dmoe)
    gathered_grads = deliver(grad_buffer, experts, slots)
    dact = jnp.einsum("erd,efd->erf", gathered_grads, w_down, preferred_element_type=jnp.float32)
    dpre = (dact * gelu_slope(pre)).astype(jnp.bfloat16)
    grad_down = jnp.einsum("erf,erd->efd", act, gathered_grads, preferred_element_type=jnp.float32)
    grad_up = jnp.einsum("erd,erf->edf", gathered, dpre, preferred_element_type=jnp.float32)
    back_partial = jnp.einsum("erf,edf->erd", dpre, w_up, preferred_element_type=jnp.float32)
    dxe = give_back(back_partial, n_dp, n_expert, slots)[dest].astype(jnp.float32)
    router_rows = jnp.dot(onehot_f, router.T, precision=lax.Precision.HIGHEST)
    gradient_normalized_input = dxe + dgl[:, None] * router_rows
    gain_partial_term = jnp.sum(gradient_normalized_input * centered_scaled_input, axis=0)
    scaled_output_gradient = gradient_normalized_input * layer_norm_gain
    normed_input_gradient = (
        scaled_output_gradient
        - jnp.mean(scaled_output_gradient, axis=1, keepdims=True)
        - centered_scaled_input
        * jnp.mean(scaled_output_gradient * centered_scaled_input, axis=1, keepdims=True)
    ) * inverse_deviation
    grad_tokens = (dy + normed_input_gradient).astype(jnp.bfloat16).reshape(pair_dev, SEQ, D)
    loss, grad_router, layer_gain_gradient = lax.psum(
        (loss_term, router_part, gain_partial_term), ("dp", "expert")
    )
    return (loss.reshape(1), grad_tokens, grad_up, grad_down, grad_router, layer_gain_gradient)


def solution(mesh):
    return jax.shard_map(
        body,
        mesh=mesh,
        in_specs=(
            P(("dp", "expert"), None, None),
            P(("dp", "expert"), None, None),
            P(("dp", "expert")),
            P(),
            P(),
            P("expert", None, "dp"),
            P("expert", "dp", None),
            P(),
            P(),
        ),
        out_specs=(
            P(),
            P(("dp", "expert"), None, None),
            P("expert", None, "dp"),
            P("expert", "dp", None),
            P(),
            P(),
        ),
        check_vma=False,
    )
```

profile of v0, /device:TPU:0, one launch (start us, length us, event | category | flops | bytes accessed | tf_op | source)
XLA Modules:
  0.0 468.2 jit_solution(15633228378693927035)
XLA Ops:
  7.2 1.3 convert_reduce_fusion
  8.5 1.3 fusion.57
  9.8 0.7 iota_compare_fusion
  11.4 0.7 fusion.69
  12.1 0.7 compare_select_fusion
  12.8 2.3 scatter_custom_fusion
  15.3 16.1 %all_to_all.16 = bf16[8,1,36,1024]{3,2,1,0:T(8,128)(2,1)S(1)} all-to-all(bf16[8,1,36,1024]{3,2,1,0:T(8,128)(2,1)S(1)} %bitcast.185), channel_id=1, replica_groups=mesh['dp'=4,'expert'=8] {'expert'}, dimensions={0} | all-to-all | bytes 1179648 | tf_op jit(solution)/shard_map/all_to_all | solution.py:25
  31.4 1.1 copy.16
  32.6 49.5 %all-gather.7.cloned.1.call-done = bf16[32,1,36,1024]{3,0,2,1:T(8,128)(2,1)} async-done(((bf16[8,1,36,1024]{3,0,2,1:T(8,128)(2,1)}), bf16[32,1,36,1024]{3,0,2,1:T(8,128)(2,1)}) %all-gather.7.cloned.1.call-update) | async-done | bytes 2359312 | tf_op jit(solution)/shard_map/all_gather | solution.py:29
  82.1 4.5 copy.17
  86.5 4.1 reshape.516
  90.7 14.6 %fusion.2 = (bf16[1152,1024]{1,0:T(8,128)(2,1)S(1)}, f32[1152,1024]{1,0:T(8,128)}) fusion(bf16[1152,1024]{1,0:T(8,128)(2,1)} %reshape.516, bf16[1,1024,1024]{2,1,0:T(8,128)(2,1)S(1)} %copy-done), kind=kOutput, calls=%fused_computation.9 | convolution fusion | flops 2492596224 | bytes 11534336 | tf_op jit(solution)/shard_map/erd,edf->erf/dot_general | solution.py:78
  105.3 1.5 copy-done.8
  106.7 3.8 convert_bitcast_fusion.1
  111.5 45.7 %reduce-scatter.3.cloned.1.call-done = bf16[1,1,288,1024]{3,2,1,0:T(8,128)(2,1)} async-done(((bf16[1,4,288,1024]{3,2,1,0:T(8,128)(2,1)}), bf16[1,1,288,1024]{3,2,1,0:T(8,128)(2,1)}) %reduce-scatter.3.cloned.1.call-update) | async-done | bytes 589840 | tf_op jit(solution)/shard_map/reduce_scatter | solution.py:36
  157.2 2.0 reshape.519
  159.2 4.2 all-to-all-start.1
  165.3 9.2 %all-to-all-done.1 = bf16[1,8,36,1024]{3,2,0,1:T(8,128)(2,1)} async-done(((bf16[1,8,36,1024]{3,2,0,1:T(8,128)(2,1)}), bf16[1,8,36,1024]{3,2,0,1:T(8,128)(2,1)}, u32[]{:S(2)}, u32[]{:S(2)}) %all-to-all-start.1) | async-done | bytes 589856 | tf_op jit(solution)/shard_map/all_to_all | solution.py:43
  174.6 1.2 reshape.520
  175.8 1.8 gather_fusion
  177.6 1.2 convert_add_fusion
  181.6 38.6 %all-gather.1 = f32[32768]{0:T(1024)S(1)} all-gather(f32[1024]{0:T(1024)S(1)} %broadcast_divide_fusion), channel_id=3, replica_groups=mesh['dp'=4,'expert'=8] {'dp','expert'}, dimensions={0}, use_global_device_ids=true | all-gather | bytes 135168 | tf_op jit(solution)/shard_map/all_gather | solution.py:103
  220.2 37.2 %all-gather.2 = f32[32768]{0:T(1024)S(1)} all-gather(f32[1024]{0:T(1024)S(1)} %multiply_divide_fusion), channel_id=4, replica_groups=mesh['dp'=4,'expert'=8] {'dp','expert'}, dimensions={0}, use_global_device_ids=true | all-gather | bytes 135168 | tf_op jit(solution)/shard_map/all_gather | solution.py:102
  257.4 0.8 fusion.79
  258.4 0.6 multiply_reduce_fusion.2
  261.6 2.4 scatter_custom_fusion.1
  264.0 2.0 reshape.523
  266.0 14.6 %all_to_all.17 = bf16[8,1,36,1024]{3,2,1,0:T(8,128)(2,1)S(1)} all-to-all(bf16[8,1,36,1024]{3,2,1,0:T(8,128)(2,1)} %bitcast.186), channel_id=1, replica_groups=mesh['dp'=4,'expert'=8] {'expert'}, dimensions={0} | all-to-all | bytes 1179648 | tf_op jit(solution)/shard_map/all_to_all | solution.py:25
  280.6 1.1 copy.20
  281.8 46.4 %all-gather.9.cloned.1.call-done = bf16[32,1,36,1024]{3,0,2,1:T(8,128)(2,1)} async-done(((bf16[8,1,36,1024]{3,0,2,1:T(8,128)(2,1)}), bf16[32,1,36,1024]{3,0,2,1:T(8,128)(2,1)}) %all-gather.9.cloned.1.call-update) | async-done | bytes 2359312 | tf_op jit(solution)/shard_map/all_gather | solution.py:29
  328.2 4.5 copy.21
  332.7 4.1 reshape.525
  336.8 6.9 %fusion.14 = bf16[1152,1024]{1,0:T(8,128)(2,1)S(1)} fusion(f32[1152,1024]{1,0:T(8,128)} %get-tuple-element.13, bf16[1152,1024]{1,0:T(8,128)(2,1)} %reshape.525, bf16[1,1024,1024]{2,1,0:T(8,128)(2,1)} %param.15), kind=kOutput, calls=%fused_computation.29 | convolution fusion | flops 2427715584 | bytes 11534336 | tf_op jit(solution)/shard_map/erd,efd->erf/dot_general | solution.py:125
  343.6 1.4 copy-done.9
  345.0 3.9 convert_bitcast_fusion
  349.6 1.2 fusion.42
  350.9 1.3 fusion.70
  352.2 7.7 %convolution_bitcast_fusion = f32[1,1024,1024]{2,1,0:T(8,128)} fusion(bf16[1152,1024]{1,0:T(8,128)(2,1)} %copy-done.8, bf16[1152,1024]{1,0:T(8,128)(2,1)} %reshape.525), kind=kOutput, calls=%fused_computation.32 | convolution fusion | flops 2415919104 | bytes 8912896 | tf_op jit(solution)/shard_map/erf,erd->efd/dot_general | solution.py:127
  359.9 35.7 %reduce-scatter.5.cloned.1.call-done = bf16[1,1,288,1024]{3,2,1,0:T(8,128)(2,1)} async-done(((bf16[1,4,288,1024]{3,2,1,0:T(8,128)(2,1)}), bf16[1,1,288,1024]{3,2,1,0:T(8,128)(2,1)}) %reduce-scatter.5.cloned.1.call-update) | async-done | bytes 589840 | tf_op jit(solution)/shard_map/reduce_scatter | solution.py:36
  395.6 2.0 reshape.526
  397.6 4.4 all-to-all-start.3
  402.1 7.3 %convolution_bitcast_fusion.1 = f32[1,1024,1024]{2,1,0:T(8,128)} fusion(bf16[1152,1024]{1,0:T(8,128)(2,1)} %reshape.516, bf16[1152,1024]{1,0:T(8,128)(2,1)} %copy-done.9), kind=kOutput, calls=%fused_computation.33 | convolution fusion | flops 2415919104 | bytes 8912896 | tf_op jit(solution)/shard_map/erd,erf->edf/dot_general | solution.py:128
  409.4 3.6 all-to-all-done.3
  413.0 1.2 reshape.527
  414.2 1.8 gather_fusion.1
  416.0 3.1 fusion.56
  419.1 40.1 %all-reduce.1 = (f32[1]{0:T(128)}, f32[1024,8]{0,1:T(8,128)}, f32[1024]{0:T(1024)}) all-reduce(f32[1]{0:T(128)} %bitcast.22, f32[1024,8]{0,1:T(8,128)S(1)} %fusion.70, f32[1024]{0:T(1024)S(1)} %get-tuple-element.6), channel_id=1, replica_groups=mesh['dp'=4,'expert'=8] {'dp','expert'}, use_global_device_ids=true, to_apply=%region_13.14 | all-reduce | flops 9217 | bytes 73736 | tf_op jit(solution)/shard_map/psum | solution.py:142
  459.2 2.5 fusion.63
  (58 shorter events, 4.8 us)
Async XLA Ops:
  7.2 83.5 %copy-start = (bf16[1,1024,1024]{2,1,0:T(8,128)(2,1)S(1)}, bf16[1,1024,1024]{2,1,0:T(8,128)(2,1)}, u32[]{:S(2)}) copy-start(bf16[1,1024,1024]{2,1,0:T(8,128)(2,1)} %param.14) | copy-start | bytes 6291460
  7.2 74.9 %all-gather.7.cloned.1.call-start = ((), (), s32[]{:S(2)}) async-start(), calls=%async_computation.8 | async-start | bytes 2949120 | tf_op jit(solution)/shard_map/all_gather | solution.py:29
  32.6 124.7 %reduce-scatter.3.cloned.1.call-start = ((), (), s32[]{:S(2)}) async-start(), calls=%async_computation.6 | async-start | bytes 2949120 | tf_op jit(solution)/shard_map/reduce_scatter | solution.py:36
  90.6 16.1 %copy-start.7 = (bf16[1,1024,1024]{2,1,0:T(8,128)(2,1)S(1)}, bf16[1,1024,1024]{2,1,0:T(8,128)(2,1)}, u32[]{:S(2)}) copy-start(bf16[1,1024,1024]{2,1,0:T(8,128)(2,1)} %param.15) | copy-start | bytes 6291460
  105.3 1.5 copy-start.8
  106.7 4.5 copy-start.1
  106.7 4.5 copy-start.4
  110.6 54.3 %copy-start.5 = (f32[1024,8]{0,1:T(8,128)S(1)}, f32[1024,8]{0,1:T(8,128)}, u32[]{:S(2)}) copy-start(f32[1024,8]{0,1:T(8,128)} %param.13) | copy-start | bytes 98308
  110.6 54.3 %copy-start.6 = (s32[1,212,1]{1,2,0:T(1,128)S(1)}, s32[1,212,1]{1,2,0:T(1,128)}, u32[]{:S(2)}) copy-start(s32[1,212,1]{1,2,0:T(1,128)} %param.10) | copy-start | bytes 2548
  111.5 53.8 %copy-start.3 = (bf16[212,1024]{1,0:T(8,128)(2,1)}, bf16[212,1024]{1,0:T(8,128)(2,1)S(1)}, u32[]{:S(2)}) copy-start(bf16[212,1024]{1,0:T(8,128)(2,1)S(1)} %fusion.50) | copy-start | bytes 1302532
  159.2 15.3 %all-to-all-start.1 = ((bf16[1,8,36,1024]{3,2,0,1:T(8,128)(2,1)}), bf16[1,8,36,1024]{3,2,0,1:T(8,128)(2,1)}, u32[]{:S(2)}, u32[]{:S(2)}) async-start(bf16[1,8,36,1024]{3,2,0,1:T(8,128)(2,1)} %bitcast.184), calls=%async_computation.2 | async-start | bytes 1310720 | tf_op jit(solution)/shard_map/all_to_all | solution.py:43
  163.4 164.8 %all-gather.9.cloned.1.call-start = ((), (), s32[]{:S(2)}) async-start(), calls=%async_computation.9 | async-start | bytes 2949120 | tf_op jit(solution)/shard_map/all_gather | solution.py:29
  261.6 88.0 %copy-start.2 = (f32[1,196,1024]{2,1,0:T(8,128)}, f32[1,196,1024]{2,1,0:T(8,128)S(1)}, u32[]{:S(2)}) copy-start(f32[1,196,1024]{2,1,0:T(8,128)S(1)} %broadcast_in_dim.10) | copy-start | bytes 2408452
  281.8 113.9 %reduce-scatter.5.cloned.1.call-start = ((), (), s32[]{:S(2)}) async-start(), calls=%async_computation.7 | async-start | bytes 2949120 | tf_op jit(solution)/shard_map/reduce_scatter | solution.py:36
  343.6 1.4 copy-start.9
  397.6 15.3 %all-to-all-start.3 = ((bf16[1,8,36,1024]{3,2,0,1:T(8,128)(2,1)}), bf16[1,8,36,1024]{3,2,0,1:T(8,128)(2,1)}, u32[]{:S(2)}, u32[]{:S(2)}) async-start(bf16[1,8,36,1024]{3,2,0,1:T(8,128)(2,1)} %bitcast.34), calls=%async_computation.5 | async-start | bytes 1310720 | tf_op jit(solution)/shard_map/all_to_all | solution.py:43
Sparse Core Ops, SparseCore 0:
  32.7 49.3 all-gather.6
  110.7 46.4 reduce-scatter.2
  281.9 46.2 all-gather.8
  349.1 46.4 reduce-scatter.4
where the time goes:
time: 470 us; the launch traced here: 468 us
  waiting for transfers between devices  190 us (40%)
  blocking collectives  147 us (31%)
  matrix products  50.6 us (11%)
  local copies, waits for them, and re-layouts  34.9 us (7%)
  between operations  19.4 us (4%)
  other arithmetic  18 us (4%)
  starting transfers between devices  8.79 us (2%)
    all_gather x2, waiting for transfers between devices, deliver(): whole = lax.all_gather(shaped, 'dp', axis=1, tiled=True)  95.9 us
    reduce_scatter x2, waiting for transfers between devices, give_back(): lax.psum_scatter(partial_value.reshape(local, n_dp, n_expert * slots, wid...  81.4 us
    psum x1, blocking collectives, body(): lax.psum((loss_term, router_part, gain_partial_term), ('dp', 'expert'))  40.1 us
    all_gather x1, blocking collectives, body(): lax.all_gather(v, ('dp', 'expert'), axis=0, tiled=True)  38.6 us
    all_gather x1, blocking collectives, body(): lax.all_gather(u, ('dp', 'expert'), axis=0, tiled=True)  37.2 us
    all_to_all x2, blocking collectives, deliver(): lax.all_to_all(buffer.reshape(experts, 1, slots, width), 'expert', split_...  30.7 us
    dot_general x1, matrix products, body(): jnp.einsum('erd,edf->erf', gathered, w_up, preferred_element_type=jnp.flo...  14.6 us
    all_to_all x2, waiting for transfers between devices, give_back(): lax.all_to_all(rounded, 'expert', split_axis=1, concat_axis=0, tiled=True)  12.8 us
  transfers between devices with their start and end apart: 6, of which 6 were waited for; matrix products, arithmetic and copies ran while one was open for 4% of the time, Pallas kernels for 0%

commit v1 on v0

v1 whole, which is shorter than its diff:
```python
import functools

import jax
import jax.numpy as jnp
from jax import lax
from jax.experimental import pallas as pl
from jax.experimental.pallas import tpu as pltpu
from jax.sharding import PartitionSpec as P

D = 1024
PATCH = 196
CAPLEN = 16
SEQ = 212

eps = 1e-06
loss_scale = 1024.0
MESH = pl.DeviceIdType.MESH
HIGHEST = lax.Precision.HIGHEST


def gelu_slope(pre):
    return (
        0.5 * (1.0 + lax.erf(pre * 0.7071067811865476))
        + pre * jnp.exp(-0.5 * pre * pre) * 0.3989422804014327
    )


def split(value):
    high = lax.reduce_precision(value, 8, 7)
    return high.astype(jnp.bfloat16), (value - high).astype(jnp.bfloat16)


def dot(a, b, contract):
    return lax.dot_general(a, b, (contract, ((), ())), preferred_element_type=jnp.float32)


def vmem():
    return pl.BlockSpec(memory_space=pltpu.VMEM)


def dispatch_kernel(nd, ne, x_ref, out_ref, own_sem, a_sem, up_sem, dn_sem, r_sem):
    z = lax.axis_index("dp")
    e = lax.axis_index("expert")

    def hop(o, s, step, sem):
        return pltpu.make_async_remote_copy(
            src_ref=out_ref.at[o, s],
            dst_ref=out_ref.at[o, s],
            send_sem=sem.at[o, s],
            recv_sem=r_sem.at[o, s],
            device_id=(z + step, e),
            device_id_type=MESH,
        )

    def cross(t):
        return pltpu.make_async_remote_copy(
            src_ref=x_ref.at[t],
            dst_ref=out_ref.at[z, e],
            send_sem=a_sem.at[t],
            recv_sem=r_sem.at[z, e],
            device_id=(z, t),
            device_id_type=MESH,
        )

    def forward_up(o, s):
        @pl.when(z < nd - 1)
        def _():
            hop(o, s, 1, up_sem).start()

    def forward_dn(o, s):
        @pl.when(z > 0)
        def _():
            hop(o, s, -1, dn_sem).start()

    own = pltpu.make_async_copy(x_ref.at[e], out_ref.at[z, e], own_sem)
    own.start()

    @pl.loop(1, ne)
    def _(k):
        cross(lax.rem(e + k, ne)).start()

    own.wait()
    forward_up(z, e)
    forward_dn(z, e)

    @pl.loop(1, ne)
    def _(k):
        s = lax.rem(e + ne - k, ne)
        hop(z, s, 0, up_sem).wait_recv()
        forward_up(z, s)
        forward_dn(z, s)

    for d in range(1, nd):

        @pl.loop(0, ne)
        def _(k):
            s = lax.rem(e + ne - k, ne)

            @pl.when(z - d >= 0)
            def _():
                hop(z - d, s, 0, up_sem).wait_recv()
                forward_up(z - d, s)

            @pl.when(z + d < nd)
            def _():
                hop(z + d, s, 0, up_sem).wait_recv()
                forward_dn(z + d, s)

    @pl.loop(1, ne)
    def _(k):
        cross(lax.rem(e + k, ne)).wait_send()

    @pl.loop(0, nd)
    def _(o):
        @pl.loop(0, ne)
        def _(s):
            @pl.when((z < nd - 1) & (o <= z))
            def _():
                hop(o, s, 0, up_sem).wait_send()

            @pl.when((z > 0) & (o >= z))
            def _():
                hop(o, s, 0, dn_sem).wait_send()


def dispatch(buffer, nd, ne):
    _, height, width = buffer.shape
    return pl.pallas_call(
        functools.partial(dispatch_kernel, nd, ne),
        out_shape=jax.ShapeDtypeStruct((nd, ne, height, width), buffer.dtype),
        in_specs=[vmem()],
        out_specs=vmem(),
        scratch_shapes=[
            pltpu.SemaphoreType.DMA,
            pltpu.SemaphoreType.DMA((ne,)),
            pltpu.SemaphoreType.DMA((nd, ne)),
            pltpu.SemaphoreType.DMA((nd, ne)),
            pltpu.SemaphoreType.DMA((nd, ne)),
        ],
        compiler_params=pltpu.CompilerParams(has_side_effects=True),
        name="dispatch",
    )(buffer)


def bring_kernel(
    nd, ne, b_ref, ret_ref, from_dn, from_up, fin, up_sem, dn_sem, ru_sem, rd_sem, a_sem, ra_sem
):
    z = lax.axis_index("dp")
    e = lax.axis_index("expert")

    def rise(src, o, s):
        return pltpu.make_async_remote_copy(
            src_ref=src.at[o, s],
            dst_ref=from_dn.at[o, s],
            send_sem=up_sem.at[o, s],
            recv_sem=ru_sem.at[o, s],
            device_id=(z + 1, e),
            device_id_type=MESH,
        )

    def fall(src, o, s):
        return pltpu.make_async_remote_copy(
            src_ref=src.at[o, s],
            dst_ref=from_up.at[o, s],
            send_sem=dn_sem.at[o, s],
            recv_sem=rd_sem.at[o, s],
            device_id=(z - 1, e),
            device_id_type=MESH,
        )

    def cross(s):
        return pltpu.make_async_remote_copy(
            src_ref=fin.at[s],
            dst_ref=ret_ref.at[e],
            send_sem=a_sem.at[s],
            recv_sem=ra_sem.at[e],
            device_id=(z, s),
            device_id_type=MESH,
        )

    def back(s):
        return pltpu.make_async_remote_copy(
            src_ref=fin.at[s],
            dst_ref=ret_ref.at[s],
            send_sem=a_sem.at[s],
            recv_sem=ra_sem.at[s],
            device_id=(z, s),
            device_id_type=MESH,
        )

    def add(held, o, s):
        total = held[o, s].astype(jnp.float32) + b_ref[o, s].astype(jnp.float32)
        held[o, s] = total.astype(held.dtype)

    for j in range(nd - 1):
        high, low = nd - 1 - j, j

        @pl.loop(0, ne)
        def _(k):
            s = lax.rem(e + k + 1, ne)

            @pl.when((high > z) & (z == 0))
            def _():
                rise(b_ref, high, s).start()

            @pl.when((high > z) & (z > 0))
            def _():
                rise(from_dn, high, s).wait_recv()
                add(from_dn, high, s)
                rise(from_dn, high, s).start()

            @pl.when((low < z) & (z == nd - 1))
            def _():
                fall(b_ref, low, s).start()

            @pl.when((low < z) & (z < nd - 1))
            def _():
                fall(from_up, low, s).wait_recv()
                add(from_up, low, s)
                fall(from_up, low, s).start()

    @pl.loop(0, ne)
    def _(k):
        s = lax.rem(e + k + 1, ne)
        fin[s] = b_ref[z, s]

        @pl.when(z > 0)
        def _():
            rise(from_dn, z, s).wait_recv()
            fin[s] = (fin[s].astype(jnp.float32) + from_dn[z, s].astype(jnp.float32)).astype(
                fin.dtype
            )

        @pl.when(z < nd - 1)
        def _():
            fall(from_up, z, s).wait_recv()
            fin[s] = (fin[s].astype(jnp.float32) + from_up[z, s].astype(jnp.float32)).astype(
                fin.dtype
            )

        @pl.when(s != e)
        def _():
            cross(s).start()

        @pl.when(s == e)
        def _():
            ret_ref[e] = fin[e]

    @pl.loop(1, ne)
    def _(k):
        back(lax.rem(e + ne - k, ne)).wait_recv()

    @pl.loop(1, ne)
    def _(k):
        cross(lax.rem(e + k, ne)).wait_send()

    @pl.loop(0, nd)
    def _(o):
        @pl.loop(0, ne)
        def _(s):
            @pl.when(o > z)
            def _():
                rise(b_ref, o, s).wait_send()

            @pl.when(o < z)
            def _():
                fall(b_ref, o, s).wait_send()


def bring_back(partial_rows, nd, ne):
    _, _, height, width = partial_rows.shape
    dtype = partial_rows.dtype
    dma = pltpu.SemaphoreType.DMA
    return pl.pallas_call(
        functools.partial(bring_kernel, nd, ne),
        out_shape=jax.ShapeDtypeStruct((ne, height, width), dtype),
        in_specs=[vmem()],
        out_specs=vmem(),
        scratch_shapes=[
            pltpu.VMEM((nd, ne, height, width), dtype),
            pltpu.VMEM((nd, ne, height, width), dtype),
            pltpu.VMEM((ne, height, width), dtype),
            dma((nd, ne)),
            dma((nd, ne)),
            dma((nd, ne)),
            dma((nd, ne)),
            dma((ne,)),
            dma((ne,)),
        ],
        compiler_params=pltpu.CompilerParams(has_side_effects=True),
        name="bring_back",
    )(partial_rows)


def spread(nd, ne, me, src, dst, send_sem, recv_sem):
    n = nd * ne

    def copy(t, sender):
        return pltpu.make_async_remote_copy(
            src_ref=src(t),
            dst_ref=dst.at[sender],
            send_sem=send_sem.at[t],
            recv_sem=recv_sem.at[sender],
            device_id=(t // ne, lax.rem(t, ne)),
            device_id_type=MESH,
        )

    @pl.loop(1, n)
    def _(k):
        copy(lax.rem(me + k, n), me).start()

    @pl.loop(1, n)
    def _(k):
        t = lax.rem(me + n - k, n)
        copy(t, t).wait_recv()

    return copy


def drain(n, me, copy):
    @pl.loop(1, n)
    def _(k):
        copy(lax.rem(me + k, n), me).wait_send()


def pairs_kernel(nd, ne, m_ref, x_ref, out_ref, held, own, s1, r1, s2, r2):
    n = nd * ne
    me = lax.axis_index("dp") * ne + lax.axis_index("expert")
    held[me] = m_ref[me]
    first = spread(nd, ne, me, lambda t: m_ref.at[t], held, s1, r1)
    total = jnp.sum(held[...], axis=0) + x_ref[...]
    own[...] = total
    out_ref[me] = total
    second = spread(nd, ne, me, lambda t: own, out_ref, s2, r2)
    drain(n, me, first)
    drain(n, me, second)


def pair_sums(m, x, nd, ne):
    n = nd * ne
    dma = pltpu.SemaphoreType.DMA
    return pl.pallas_call(
        functools.partial(pairs_kernel, nd, ne),
        out_shape=jax.ShapeDtypeStruct(m.shape, m.dtype),
        in_specs=[vmem(), vmem()],
        out_specs=vmem(),
        scratch_shapes=[
            pltpu.VMEM(m.shape, m.dtype),
            pltpu.VMEM(x.shape, x.dtype),
            dma((n,)),
            dma((n,)),
            dma((n,)),
            dma((n,)),
        ],
        compiler_params=pltpu.CompilerParams(has_side_effects=True),
        name="pair_sums",
    )(m, x)


def everyone_kernel(nd, ne, x_ref, out_ref, s1, r1):
    n = nd * ne
    me = lax.axis_index("dp") * ne + lax.axis_index("expert")
    out_ref[me] = x_ref[...]
    drain(n, me, spread(nd, ne, me, lambda t: x_ref, out_ref, s1, r1))


def everyone(x, nd, ne):
    n = nd * ne
    dma = pltpu.SemaphoreType.DMA
    return pl.pallas_call(
        functools.partial(everyone_kernel, nd, ne),
        out_shape=jax.ShapeDtypeStruct((n,) + x.shape, x.dtype),
        in_specs=[vmem()],
        out_specs=vmem(),
        scratch_shapes=[dma((n,)), dma((n,))],
        compiler_params=pltpu.CompilerParams(has_side_effects=True),
        name="everyone",
    )(x)


def body(
    tokens,
    expert_ids,
    caption_lengths,
    layer_norm_gain,
    router,
    w_up,
    w_down,
    logit_scale,
    logit_bias,
):
    nd = lax.axis_size("dp")
    ne = lax.axis_size("expert")
    n = nd * ne
    assert tokens.shape[0] == 1 and w_up.shape[0] == 1
    rows = SEQ
    experts = router.shape[1]
    slots = rows * 4 // (3 * experts) + 1
    height = -(-(slots + 1) // 8) * 8
    total = n * height
    expert = lax.axis_index("expert")
    me = lax.axis_index("dp") * ne + expert
    wu, wd = w_up[0], w_down[0]

    x = tokens.reshape(rows, D).astype(jnp.float32)
    mean = jnp.mean(x, axis=1, keepdims=True)
    var = jnp.mean((x - mean) ** 2, axis=1, keepdims=True)
    rstd = 1.0 / jnp.sqrt(var + eps)
    xhat = (x - mean) * rstd
    xn = (xhat * layer_norm_gain).astype(jnp.bfloat16)

    ids = expert_ids.reshape(rows)
    onehot = ids[:, None] == jnp.arange(experts, dtype=jnp.int32)[None, :]
    earlier = jnp.arange(rows)[:, None] > jnp.arange(rows)[None, :]
    before = dot(earlier.astype(jnp.bfloat16), onehot.astype(jnp.bfloat16), ((1,), (0,)))
    slot = jnp.sum(jnp.where(onehot, before, 0.0), axis=1).astype(jnp.int32)
    dest = ids * height + slot
    place = (jnp.arange(experts * height, dtype=jnp.int32)[:, None] == dest[None, :]).astype(
        jnp.bfloat16
    )
    length = caption_lengths.astype(jnp.float32)
    row = jnp.arange(rows, dtype=jnp.int32)
    mark = jnp.where(row < PATCH, -1.0, jnp.where(row - PATCH < caption_lengths[0], length[0], 0.0))
    marks = jnp.sum(place.astype(jnp.float32) * mark[None, :], axis=1).reshape(experts, 1, height)
    marks = jnp.pad(marks, ((0, 0), (0, 0), (0, D - height)))
    packed = dot(place, xn, ((1,), (0,))).reshape(experts, height, D)
    is_mark = (jnp.arange(height) == slots)[None, :, None]
    packed = jnp.where(is_mark, marks, packed).astype(jnp.bfloat16)

    got = dispatch(packed, nd, ne)
    xe = got.reshape(total, D)

    marks = got.reshape(n, height, D)[:, slots, :height].astype(jnp.float32)
    marks = jnp.where(jnp.arange(height)[None, :] < slots, marks, 0.0).reshape(total)
    is_img, is_txt = marks < 0.0, marks > 0.0
    weight = jnp.where(is_img, 1.0 / PATCH, jnp.where(is_txt, 1.0 / jnp.maximum(marks, 1.0), 0.0))
    column = lax.dynamic_slice_in_dim(router, expert, 1, axis=1)[:, 0]
    xef = xe.astype(jnp.float32)
    gate = jax.nn.sigmoid(jnp.sum(xef * column[None, :], axis=1))
    coef_row = weight * gate
    pre = dot(xe, wu, ((1,), (0,)))
    act = jax.nn.gelu(pre, approximate=False).astype(jnp.bfloat16)
    kind = jnp.arange(2 * n, dtype=jnp.int32)[:, None]
    pair_of = jnp.arange(total, dtype=jnp.int32)[None, :] // height
    member = (kind // 2 == pair_of) & ((kind % 2 == 0) == is_img[None, :])
    q_high, q_low = split(jnp.where(member, coef_row[None, :], 0.0))
    both = dot(jnp.concatenate([q_high, q_low], axis=0), act, ((1,), (0,)))
    a = both[: 2 * n] + both[2 * n :]
    a_high, a_low = split(a)
    both = dot(jnp.concatenate([a_high, a_low], axis=0), wd, ((1,), (0,)))
    moe_sums = both[: 2 * n] + both[2 * n :]

    img_x = jnp.sum(x[:PATCH], axis=0) / PATCH
    mask = (jnp.arange(CAPLEN, dtype=jnp.int32) < caption_lengths[0]).astype(jnp.float32)
    txt_x = jnp.sum(x[PATCH:] * mask[:, None], axis=0) / length[0]
    own_x = jnp.concatenate([img_x, txt_x]).reshape(8, 2 * D // 8)
    sums = pair_sums(moe_sums.reshape(n, 8, 2 * D // 8), own_x, nd, ne).reshape(n, 2, D)
    img, txt = sums[:, 0], sums[:, 1]

    ru = jnp.sqrt(jnp.mean(img * img, axis=1, keepdims=True) + eps)
    rv = jnp.sqrt(jnp.mean(txt * txt, axis=1, keepdims=True) + eps)
    u, v = img / ru, txt / rv
    scale = logit_scale[0]
    logits = (
        scale * lax.dot_general(u, v, (((1,), (1,)), ((), ())), precision=HIGHEST) / D
        + logit_bias[0]
    )
    sign = 2.0 * jnp.eye(n, dtype=jnp.float32) - 1.0
    loss = -jnp.sum(jax.nn.log_sigmoid(sign * logits)) / n
    coef = -(loss_scale / n) * sign * jax.nn.sigmoid(-sign * logits)
    du = scale / D * jnp.dot(coef, v, precision=HIGHEST)
    dv = scale / D * lax.dot_general(coef, u, (((0,), (0,)), ((), ())), precision=HIGHEST)
    dimg = (du - u * jnp.mean(du * u, axis=1, keepdims=True)) / ru
    dtxt = (dv - v * jnp.mean(dv * v, axis=1, keepdims=True)) / rv
    dvec = jnp.stack([dimg, dtxt], axis=1).reshape(2 * n, D)
    d_high, d_low = split(dvec)

    both = dot(jnp.concatenate([d_high, d_low], axis=0), wd, ((1,), (1,)))
    dhid = (both[: 2 * n] + both[2 * n :]).reshape(n, 2, 1, -1)
    chosen = jnp.where(is_img.reshape(n, height, 1), dhid[:, 0], dhid[:, 1]).reshape(total, -1)
    dgl = jnp.sum(act.astype(jnp.float32) * chosen, axis=1) * weight * gate * (1.0 - gate)
    dpre = (coef_row[:, None] * chosen * gelu_slope(pre)).astype(jnp.bfloat16)
    back = (dot(dpre, wu, ((1,), (1,))) + dgl[:, None] * column[None, :]).astype(jnp.bfloat16)
    returned = bring_back(back.reshape(nd, ne, height, D), nd, ne)
    grad_up = dot(xe, dpre, ((0,), (0,)))[None]
    grad_down = dot(
        jnp.concatenate([a_high, a_high, a_low], axis=0),
        jnp.concatenate([d_high, d_low, d_high], axis=0),
        ((0,), (0,)),
    )[None]
    router_part = jnp.sum(xef * dgl[:, None], axis=0)

    dxn = dot(place, returned.reshape(experts * height, D), ((0,), (0,)))
    gain_part = jnp.sum(dxn * xhat, axis=0)
    g = dxn * layer_norm_gain
    normed = (
        g - jnp.mean(g, axis=1, keepdims=True) - xhat * jnp.mean(g * xhat, axis=1, keepdims=True)
    ) * rstd
    mine = lax.dynamic_slice_in_dim(dvec, 2 * me, 2, axis=0)
    dy = jnp.where(
        (row < PATCH)[:, None],
        mine[0:1] / PATCH,
        jnp.where(mark > 0.0, 1.0 / length[0], 0.0)[:, None] * mine[1:2],
    )
    grad_tokens = (dy + normed).astype(jnp.bfloat16).reshape(1, SEQ, D)
    last = everyone(jnp.concatenate([gain_part, router_part]).reshape(8, 2 * D // 8), nd, ne)
    last = last.reshape(nd, ne, 2, D)
    gain_grad = jnp.sum(last[:, :, 0], axis=(0, 1))
    grad_router = jnp.sum(last[:, :, 1], axis=0).T
    return (loss.reshape(1), grad_tokens, grad_up, grad_down, grad_router, gain_grad)


def solution(mesh):
    return jax.shard_map(
        body,
        mesh=mesh,
        in_specs=(
            P(("dp", "expert"), None, None),
            P(("dp", "expert"), None, None),
            P(("dp", "expert")),
            P(),
            P(),
            P("expert", None, "dp"),
            P("expert", "dp", None),
            P(),
            P(),
        ),
        out_specs=(
            P(),
            P(("dp", "expert"), None, None),
            P("expert", None, "dp"),
            P("expert", "dp", None),
            P(),
            P(),
        ),
        check_vma=False,
    )
```

time: 470 us -> 285 us (0.61)
  waiting for transfers between devices: 190 us -> 0 us
  Pallas kernels: 0 us -> 178 us
  blocking collectives: 147 us -> 0 us
  between operations: 19.4 us -> 5.22 us
  starting transfers between devices: 8.79 us -> 0 us
  other arithmetic: 18 us -> 25.6 us
  local copies, waits for them, and re-layouts: 34.9 us -> 27.4 us
    pallas_call x0 -> x4, Pallas kernels: none -> 178 us  [the longest x1 77.7 us: bring_back(): pl.pallas_call(functools.partial(bring_kernel, nd, ne), out_shape=jax.Sha...]
    all_gather x2 -> x0, waiting for transfers between devices: 95.9 us -> none  [deliver(): whole = lax.all_gather(shaped, 'dp', axis=1, tiled=True)]
    reduce_scatter x2 -> x0, waiting for transfers between devices: 81.4 us -> none  [give_back(): lax.psum_scatter(partial_value.reshape(local, n_dp, n_expert * slots, wid...]
    all_gather x2 -> x0, blocking collectives: 75.8 us -> none  [the longest x1 38.6 us: body(): lax.all_gather(v, ('dp', 'expert'), axis=0, tiled=True)]
    psum x1 -> x0, blocking collectives: 40.1 us -> none  [body(): lax.psum((loss_term, router_part, gain_partial_term), ('dp', 'expert'))]
    all_to_all x2 -> x0, blocking collectives: 30.7 us -> none  [deliver(): lax.all_to_all(buffer.reshape(experts, 1, slots, width), 'expert', split_...]
    broadcast_in_dim x1 -> x9, local copies, waits for them, and re-layouts: 0.08 us -> 18 us  [the longest x4 17.8 us: body(): jnp.where(is_img.reshape(n, height, 1), dhid[:, 0], dhid[:, 1])]
    all_to_all x2 -> x0, waiting for transfers between devices: 12.8 us -> none  [give_back(): lax.all_to_all(rounded, 'expert', split_axis=1, concat_axis=0, tiled=True)]
  transfers between devices with their start and end apart: 6 -> 0, of which waited for: 6 -> 0; matrix products, arithmetic and copies ran while one was open for 4% -> 0% of each run, Pallas kernels for 0% -> 0%
where the time goes in v1:
time: 285 us; the launch traced here: 283 us
  Pallas kernels  178 us (62%)
  matrix products  46.6 us (16%)
  local copies, waits for them, and re-layouts  27.4 us (10%)
  other arithmetic  25.6 us (9%)
  between operations  5.22 us (2%)
    pallas_call x1, Pallas kernels, bring_back(): pl.pallas_call(functools.partial(bring_kernel, nd, ne), out_shape=jax.Sha...  77.7 us
    pallas_call x1, Pallas kernels, dispatch(): pl.pallas_call(functools.partial(dispatch_kernel, nd, ne), out_shape=jax....  58.6 us
    dot_general x10, matrix products, dot(): lax.dot_general(a, b, (contract, ((), ())), preferred_element_type=jnp.fl...  44.8 us
    pallas_call x1, Pallas kernels, everyone(): pl.pallas_call(functools.partial(everyone_kernel, nd, ne), out_shape=jax....  21.2 us
    pallas_call x1, Pallas kernels, pair_sums(): pl.pallas_call(functools.partial(pairs_kernel, nd, ne), out_shape=jax.Sha...  20.7 us
    broadcast_in_dim x4, local copies, waits for them, and re-layouts, body(): jnp.where(is_img.reshape(n, height, 1), dhid[:, 0], dhid[:, 1])  17.8 us
    reduce_sum x1, other arithmetic, body(): jnp.sum(act.astype(jnp.float32) * chosen, axis=1) * weight * gate  7.77 us

profile of v1, /device:TPU:0, one launch (start us, length us, event | category | flops | bytes accessed | tf_op | source)
XLA Modules:
  0.0 282.9 jit_solution(5135945818489839286)
XLA Ops:
  2.1 0.6 compare_select_fusion.1
  2.7 0.9 fusion.28
  3.6 0.7 convert_add_fusion
  4.6 1.2 convert_reduce_fusion
  5.8 1.3 multiply_reduce_fusion.3
  7.1 0.5 copy-done.23
  7.6 2.4 fusion.25.x_ref
  10.0 58.6 %dispatch.1 = bf16[4,8,40,1024]{3,2,1,0:T(8,128)(2,1)} custom-call(bf16[8,40,1024]{2,1,0:T(8,128)(2,1)} %fusion.25.x_ref), custom_call_target="tpu_custom_call" | custom-call | tf_op jit(solution)/shard_map/dispatch/pallas_call | solution.py:128
  68.6 16.9 %fusion.4 = (bf16[1280,1024]{0,1:T(8,128)(2,1)}, f32[1280,1024]{0,1:T(8,128)}) fusion(bf16[1280,1024]{1,0:T(8,128)(2,1)} %bitcast.122, bf16[1,1024,1024]{2,1,0:T(8,128)(2,1)S(1)} %copy-done), kind=kOutput, calls=%fused_computation.8 | convolution fusion | flops 2769551360 | bytes 12582912 | tf_op jit(solution)/shard_map/dot_general | solution.py:34
  85.5 0.8 constant_dynamic-slice_fusion.1
  86.3 2.4 fusion
  88.7 0.6 copy-done.5
  89.5 0.9 fusion.89
  90.7 0.6 select_compare_fusion
  91.5 2.7 fusion.47
  94.3 2.1 fusion.20
  96.4 0.8 reshape.423.m_ref
  97.4 0.6 broadcast_divide_fusion
  98.0 1.3 div.175
  99.3 1.3 pad_maximum_fusion.1.x_ref
  100.6 20.7 %pair_sums.1 = f32[32,8,256]{2,1,0:T(8,128)} custom-call(f32[32,8,256]{2,1,0:T(8,128)} %reshape.423.m_ref, f32[8,256]{1,0:T(8,128)} %pad_maximum_fusion.1.x_ref), custom_call_target="tpu_custom_call" | custom-call | tf_op jit(solution)/shard_map/pair_sums/pallas_call | solution.py:342
  121.3 1.1 reshape.424
  122.4 0.2 fusion.91
  123.6 1.0 fusion.77
  125.2 0.4 multiply_reduce_fusion.6
  125.7 0.4 multiply_reduce_fusion.7
  126.3 0.2 copy.26
  126.5 0.2 reshape.426
  126.8 2.4 fusion.18
  129.2 0.8 reshape.427
  130.1 1.3 fusion.90
  131.4 3.0 %broadcast_in_dim.185 = f32[32,40,1024]{2,1,0:T(8,128)} broadcast(f32[32,1024]{1,0:T(8,128)S(1)} %bitcast.130), dimensions={0,2} | broadcast | bytes 5373952 | tf_op jit(solution)/shard_map/jit(_where)/broadcast_in_dim | solution.py:480
  134.4 6.0 %copy.27 = f32[1280,1024]{0,1:T(8,128)} copy(f32[1280,1024]{1,0:T(8,128)} %bitcast.126) | data formatting | bytes 10485760 | tf_op jit(solution)/shard_map/jit(_where)/broadcast_in_dim | solution.py:480
  140.4 2.9 %broadcast_in_dim.188 = f32[32,40,1024]{2,1,0:T(8,128)} broadcast(f32[32,1024]{1,0:T(8,128)S(1)} %bitcast.131), dimensions={0,2} | broadcast | bytes 5373952 | tf_op jit(solution)/shard_map/jit(_where)/broadcast_in_dim | solution.py:480
  143.3 5.9 %copy.28 = f32[1280,1024]{0,1:T(8,128)} copy(f32[1280,1024]{1,0:T(8,128)} %bitcast.127) | data formatting | bytes 10485760 | tf_op jit(solution)/shard_map/jit(_where)/broadcast_in_dim | solution.py:480
  149.2 7.8 %multiply_reduce_fusion = (f32[1280]{0:T(1024)S(1)}, bf16[1280,1024]{0,1:T(8,128)(2,1)S(1)}) fusion(bf16[1280,1024]{0,1:T(8,128)(2,1)} %get-tuple-element.27, f32[1280,1024]{0,1:T(8,128)} %copy.27, f32[1280,1024]{0,1:T(8,128)} %copy.28, pred[1280]{0:T(1024)(128)(4,1)S(1)} %copy-done.19, f32[1280,1024]{0,1:T(8,128)} %get-tuple-element.28, f32[1280]{0:T(1024)S(1)} %copy-done.10), kind=kLoop, calls=%fused_computation.16 | loop fusion | flops 19659520 | bytes 20983040 | tf_op jit(solution)/shard_map/reduce_sum | solution.py:481
  157.1 4.5 %add_convert_fusion = bf16[1280,1024]{1,0:T(8,128)(2,1)} fusion(bf16[1280,1024]{0,1:T(8,128)(2,1)S(1)} %get-tuple-element.12, f32[1024]{0:T(1024)S(1)} %bitcast.137, f32[1280]{0:T(1024)S(1)} %subtract_multiply_fusion.1, bf16[1,1024,1024]{2,1,0:T(8,128)(2,1)S(1)} %copy-done), kind=kOutput, calls=%fused_computation.15 | convolution fusion | flops 2688286720 | bytes 7349248 | tf_op jit(solution)/shard_map/dot_general | solution.py:34
  161.6 77.7 %bring_back.1 = bf16[8,40,1024]{2,1,0:T(8,128)(2,1)} custom-call(bf16[4,8,40,1024]{3,2,1,0:T(8,128)(2,1)} %bitcast.128), custom_call_target="tpu_custom_call" | custom-call | tf_op jit(solution)/shard_map/bring_back/pallas_call | solution.py:274
  239.4 2.6 multiply_reduce_fusion.1
  242.0 2.4 fusion.35
  244.4 7.5 %convolution_bitcast_fusion.1 = f32[1,1024,1024]{2,1,0:T(8,128)} fusion(bf16[1280,1024]{1,0:T(8,128)(2,1)} %bitcast.124, bf16[1280,1024]{0,1:T(8,128)(2,1)} %copy-done.2), kind=kOutput, calls=%fused_computation.34 | convolution fusion | flops 2684354560 | bytes 9437184 | tf_op jit(solution)/shard_map/dot_general | solution.py:34
  251.9 2.8 convolution_bitcast_fusion
  254.7 0.9 slice_convert_fusion
  255.6 2.3 fusion.1
  258.0 0.6 pad_maximum_fusion.2.x_ref
  258.6 21.2 %everyone.1 = f32[32,8,256]{2,1,0:T(8,128)} custom-call(f32[8,256]{1,0:T(8,128)} %pad_maximum_fusion.2.x_ref), custom_call_target="tpu_custom_call" | custom-call | tf_op jit(solution)/shard_map/everyone/pallas_call | solution.py:370
  279.8 1.1 reshape.431
  280.9 0.9 slice_reduce_fusion.1
  (104 shorter events, 2.1 us)
Async XLA Ops:
  0.6 67.9 %copy-start = (bf16[1,1024,1024]{2,1,0:T(8,128)(2,1)S(1)}, bf16[1,1024,1024]{2,1,0:T(8,128)(2,1)}, u32[]{:S(2)}) copy-start(bf16[1,1024,1024]{2,1,0:T(8,128)(2,1)} %param.14) | copy-start | bytes 6291460
  4.4 81.1 %copy-start.26 = (s32[212]{0:T(256)}, s32[212]{0:T(256)S(1)}, u32[]{:S(2)}) copy-start(s32[212]{0:T(256)S(1)} %convert_add_fusion) | copy-start | bytes 2548
  5.8 1.3 copy-start.17
  7.1 0.6 copy-start.23
  86.3 2.4 copy-start.15
  86.3 10.9 %copy-start.1 = (bf16[1,212,1024]{2,1,0:T(8,128)(2,1)S(1)}, bf16[1,212,1024]{2,1,0:T(8,128)(2,1)}, u32[]{:S(2)}) copy-start(bf16[1,212,1024]{2,1,0:T(8,128)(2,1)} %param.9) | copy-start | bytes 1302532
  88.7 0.6 copy-start.5
  89.4 2.1 copy-start.11
  89.4 2.0 copy-start.20
  89.5 1.9 copy-start.13
  90.5 0.9 copy-start.7
  90.5 0.9 copy-start.9
  94.2 2.1 copy-start.3
  143.3 5.9 %copy-start.10 = (f32[1280]{0:T(1024)S(1)}, f32[1280]{0:T(1024)}, u32[]{:S(2)}) copy-start(f32[1280]{0:T(1024)} %copy-done.9) | copy-start | bytes 15364
  143.3 5.9 %copy-start.19 = (pred[1280]{0:T(1024)(128)(4,1)S(1)}, pred[1280]{0:T(1024)(128)(4,1)}, u32[]{:S(2)}) copy-start(pred[1280]{0:T(1024)(128)(4,1)} %get-tuple-element.25) | copy-start | bytes 3844
  149.2 7.8 %copy-start.8 = (f32[1280]{0:T(1024)S(1)}, f32[1280]{0:T(1024)}, u32[]{:S(2)}) copy-start(f32[1280]{0:T(1024)} %copy-done.7) | copy-start | bytes 15364
  149.2 7.8 %copy-start.12 = (f32[1280]{0:T(1024)S(1)}, f32[1280]{0:T(1024)}, u32[]{:S(2)}) copy-start(f32[1280]{0:T(1024)} %copy-done.11) | copy-start | bytes 15364
  149.2 7.8 %copy-start.14 = (pred[1280]{0:T(1024)(128)(4,1)S(1)}, pred[1280]{0:T(1024)(128)(4,1)}, u32[]{:S(2)}) copy-start(pred[1280]{0:T(1024)(128)(4,1)} %copy-done.13) | copy-start | bytes 3844
  149.2 7.8 %copy-start.16 = (f32[1024,1]{0,1:T(1,128)S(1)}, f32[1024,1]{0,1:T(1,128)}, u32[]{:S(2)}) copy-start(f32[1024,1]{0,1:T(1,128)} %copy-done.15) | copy-start | bytes 12292
  157.0 4.6 %copy-start.2 = (bf16[1280,1024]{0,1:T(8,128)(2,1)}, bf16[1280,1024]{0,1:T(8,128)(2,1)S(1)}, u32[]{:S(2)}) copy-start(bf16[1280,1024]{0,1:T(8,128)(2,1)S(1)} %get-tuple-element.12) | copy-start | bytes 7864324
  157.1 82.3 %copy-start.18 = (f32[212]{0:T(256)S(1)}, f32[212]{0:T(256)}, u32[]{:S(2)}) copy-start(f32[212]{0:T(256)} %copy-done.17) | copy-start | bytes 2548
  157.1 82.3 %copy-start.24 = (f32[212]{0:T(256)S(1)}, f32[212]{0:T(256)}, u32[]{:S(2)}) copy-start(f32[212]{0:T(256)} %copy-done.23) | copy-start | bytes 2548
  157.1 82.3 %copy-start.25 = (f32[1024]{0:T(1024)S(1)}, f32[1024]{0:T(1024)}, u32[]{:S(2)}) copy-start(f32[1024]{0:T(1024)} %param.12) | copy-start | bytes 12292
  157.1 82.3 %copy-start.27 = (s32[212]{0:T(256)S(1)}, s32[212]{0:T(256)}, u32[]{:S(2)}) copy-start(s32[212]{0:T(256)} %copy-done.26) | copy-start | bytes 2548
  161.6 80.4 %copy-start.22 = (f32[212]{0:T(256)S(1)}, f32[212]{0:T(256)}, u32[]{:S(2)}) copy-start(f32[212]{0:T(256)} %get-tuple-element.36) | copy-start | bytes 2548
  244.3 7.5 %copy-start.4 = (bf16[64,1024]{1,0:T(8,128)(2,1)S(1)}, bf16[64,1024]{1,0:T(8,128)(2,1)}, u32[]{:S(2)}) copy-start(bf16[64,1024]{1,0:T(8,128)(2,1)} %copy-done.3) | copy-start | bytes 393220
  244.3 11.2 %copy-start.6 = (f32[4,8,40]{2,1,0:T(8,128)S(1)}, f32[4,8,40]{2,1,0:T(8,128)}, u32[]{:S(2)}) copy-start(f32[4,8,40]{2,1,0:T(8,128)} %copy-done.5) | copy-start | bytes 15364
  244.4 11.2 %copy-start.21 = (pred[40]{0:T(512)(128)(4,1)S(1)}, pred[40]{0:T(512)(128)(4,1)}, u32[]{:S(2)}) copy-start(pred[40]{0:T(512)(128)(4,1)} %copy-done.20) | copy-start | bytes 124

commit v2 on v1

--- a/solution.py
+++ b/solution.py
@@ -18,18 +18,16 @@
 HIGHEST = lax.Precision.HIGHEST
 
 
-def gelu_slope(pre):
-    return (
-        0.5 * (1.0 + lax.erf(pre * 0.7071067811865476))
-        + pre * jnp.exp(-0.5 * pre * pre) * 0.3989422804014327
-    )
-
-
 def split(value):
     high = lax.reduce_precision(value, 8, 7)
     return high.astype(jnp.bfloat16), (value - high).astype(jnp.bfloat16)
 
 
+def split3(value):
+    high = lax.reduce_precision(value, 8, 7)
+    return (high.astype(jnp.bfloat16),) + split(value - high)
+
+
 def dot(a, b, contract):
     return lax.dot_general(a, b, (contract, ((), ())), preferred_element_type=jnp.float32)
 
@@ -38,7 +36,13 @@
     return pl.BlockSpec(memory_space=pltpu.VMEM)
 
 
-def dispatch_kernel(nd, ne, x_ref, out_ref, own_sem, a_sem, up_sem, dn_sem, r_sem):
+def dispatch_kernel(
+    nd, ne, x_ref, w_ref, out_ref, act_ref, slope_ref, own_sem, a_sem, up_sem, dn_sem, r_sem
+):
+    _, height, width = x_ref.shape
+    hidden = w_ref.shape[1]
+    tiles = hidden // 128
+    every = ne // tiles
     z = lax.axis_index("dp")
     e = lax.axis_index("expert")
 
@@ -72,6 +76,28 @@
         def _():
             hop(o, s, -1, dn_sem).start()
 
+    def compute(o, k):
+        cols = pl.ds(pl.multiple_of(k // every * 128, 128), 128)
+        xe = out_ref[o].reshape(ne * height, width)
+        pre = jnp.dot(xe, w_ref[:, cols], preferred_element_type=jnp.float32)
+        half = 0.5 * (1.0 + lax.erf(pre * 0.7071067811865476))
+        bell = jnp.exp(-0.5 * pre * pre) * 0.3989422804014327
+        act_ref[o, :, cols] = (pre * half).astype(jnp.bfloat16)
+        slope_ref[o, :, cols] = half + pre * bell
+
+    def compute_ring(d, k):
+        @pl.when(lax.rem(k, every) == 0)
+        def _():
+            @pl.when(z - d >= 0)
+            def _():
+                compute(z - d, k)
+
+            if d > 0:
+
+                @pl.when(z + d < nd)
+                def _():
+                    compute(z + d, k)
+
     own = pltpu.make_async_copy(x_ref.at[e], out_ref.at[z, e], own_sem)
     own.start()
 
@@ -105,6 +131,12 @@
             def _():
                 hop(z + d, s, 0, up_sem).wait_recv()
                 forward_dn(z + d, s)
+
+            compute_ring(d - 1, k)
+
+    @pl.loop(0, ne)
+    def _(k):
+        compute_ring(nd - 1, k)
 
     @pl.loop(1, ne)
     def _(k):
@@ -123,13 +155,18 @@
                 hop(o, s, 0, dn_sem).wait_send()
 
 
-def dispatch(buffer, nd, ne):
+def dispatch(buffer, weights, nd, ne):
     _, height, width = buffer.shape
+    hidden = weights.shape[1]
     return pl.pallas_call(
         functools.partial(dispatch_kernel, nd, ne),
-        out_shape=jax.ShapeDtypeStruct((nd, ne, height, width), buffer.dtype),
-        in_specs=[vmem()],
-        out_specs=vmem(),
+        out_shape=(
+            jax.ShapeDtypeStruct((nd, ne, height, width), buffer.dtype),
+            jax.ShapeDtypeStruct((nd, ne * height, hidden), jnp.bfloat16),
+            jax.ShapeDtypeStruct((nd, ne * height, hidden), jnp.float32),
+        ),
+        in_specs=[vmem(), vmem()],
+        out_specs=(vmem(), vmem(), vmem()),
         scratch_shapes=[
             pltpu.SemaphoreType.DMA,
             pltpu.SemaphoreType.DMA((ne,)),
@@ -139,12 +176,31 @@
         ],
         compiler_params=pltpu.CompilerParams(has_side_effects=True),
         name="dispatch",
-    )(buffer)
+    )(buffer, weights)
 
 
 def bring_kernel(
-    nd, ne, b_ref, ret_ref, from_dn, from_up, fin, up_sem, dn_sem, ru_sem, rd_sem, a_sem, ra_sem
+    nd,
+    ne,
+    b_ref,
+    x_ref,
+    dpre_ref,
+    a_ref,
+    d_ref,
+    ret_ref,
+    gup_ref,
+    gdn_ref,
+    from_dn,
+    from_up,
+    fin,
+    up_sem,
+    dn_sem,
+    ru_sem,
+    rd_sem,
+    a_sem,
+    ra_sem,
 ):
+    window = min(4, ne)
     z = lax.axis_index("dp")
     e = lax.axis_index("expert")
 
@@ -188,6 +244,29 @@
             device_id_type=MESH,
         )
 
+    def place(t):
+        return lax.rem(e + lax.rem(t, ne) + 1, ne)
+
+    def risen(t):
+        rise(b_ref, nd - 1 - t // ne, place(t)).wait_send()
+
+    def fallen(t):
+        fall(b_ref, t // ne, place(t)).wait_send()
+
+    def weights(left, right, out, k):
+        tiles = left.shape[1] // 128
+        every = ne // tiles
+
+        @pl.when(lax.rem(k, every) == 0)
+        def _():
+            cols = pl.ds(pl.multiple_of(k // every * 128, 128), 128)
+            out[cols, :] = lax.dot_general(
+                left[:, cols],
+                right[...],
+                (((0,), (0,)), ((), ())),
+                preferred_element_type=jnp.float32,
+            )
+
     def add(held, o, s):
         total = held[o, s].astype(jnp.float32) + b_ref[o, s].astype(jnp.float32)
         held[o, s] = total.astype(held.dtype)
@@ -198,6 +277,15 @@
         @pl.loop(0, ne)
         def _(k):
             s = lax.rem(e + k + 1, ne)
+            t = j * ne + k
+
+            @pl.when((high > z) & (t >= window))
+            def _():
+                risen(t - window)
+
+            @pl.when((low < z) & (t >= window))
+            def _():
+                fallen(t - window)
 
             @pl.when((high > z) & (z == 0))
             def _():
@@ -218,6 +306,11 @@
                 fall(from_up, low, s).wait_recv()
                 add(from_up, low, s)
                 fall(from_up, low, s).start()
+
+            if j == 0:
+                weights(x_ref, dpre_ref, gup_ref, k)
+            if j == min(1, nd - 2):
+                weights(a_ref, d_ref, gdn_ref, k)
 
     @pl.loop(0, ne)
     def _(k):
@@ -254,28 +347,30 @@
     def _(k):
         cross(lax.rem(e + k, ne)).wait_send()
 
-    @pl.loop(0, nd)
-    def _(o):
-        @pl.loop(0, ne)
-        def _(s):
-            @pl.when(o > z)
-            def _():
-                rise(b_ref, o, s).wait_send()
-
-            @pl.when(o < z)
-            def _():
-                fall(b_ref, o, s).wait_send()
-
-
-def bring_back(partial_rows, nd, ne):
+    @pl.loop(0, window)
+    def _(i):
+        @pl.when(z < nd - 1)
+        def _():
+            risen((nd - 1 - z) * ne - window + i)
+
+        @pl.when(z > 0)
+        def _():
+            fallen(z * ne - window + i)
+
+
+def bring_back(partial_rows, xe, dpre, a, d, nd, ne):
     _, _, height, width = partial_rows.shape
     dtype = partial_rows.dtype
     dma = pltpu.SemaphoreType.DMA
     return pl.pallas_call(
         functools.partial(bring_kernel, nd, ne),
-        out_shape=jax.ShapeDtypeStruct((ne, height, width), dtype),
-        in_specs=[vmem()],
-        out_specs=vmem(),
+        out_shape=(
+            jax.ShapeDtypeStruct((ne, height, width), dtype),
+            jax.ShapeDtypeStruct((xe.shape[1], dpre.shape[1]), jnp.float32),
+            jax.ShapeDtypeStruct((a.shape[1], d.shape[1]), jnp.float32),
+        ),
+        in_specs=[vmem()] * 5,
+        out_specs=(vmem(), vmem(), vmem()),
         scratch_shapes=[
             pltpu.VMEM((nd, ne, height, width), dtype),
             pltpu.VMEM((nd, ne, height, width), dtype),
@@ -289,7 +384,7 @@
         ],
         compiler_params=pltpu.CompilerParams(has_side_effects=True),
         name="bring_back",
-    )(partial_rows)
+    )(partial_rows, xe, dpre, a, d)
 
 
 def spread(nd, ne, me, src, dst, send_sem, recv_sem):
@@ -427,19 +522,18 @@
     is_mark = (jnp.arange(height) == slots)[None, :, None]
     packed = jnp.where(is_mark, marks, packed).astype(jnp.bfloat16)
 
-    got = dispatch(packed, nd, ne)
+    got, act, slope = dispatch(packed, wu, nd, ne)
+    act, slope = act.reshape(total, -1), slope.reshape(total, -1)
     xe = got.reshape(total, D)
 
     marks = got.reshape(n, height, D)[:, slots, :height].astype(jnp.float32)
     marks = jnp.where(jnp.arange(height)[None, :] < slots, marks, 0.0).reshape(total)
     is_img, is_txt = marks < 0.0, marks > 0.0
     weight = jnp.where(is_img, 1.0 / PATCH, jnp.where(is_txt, 1.0 / jnp.maximum(marks, 1.0), 0.0))
-    column = lax.dynamic_slice_in_dim(router, expert, 1, axis=1)[:, 0]
-    xef = xe.astype(jnp.float32)
-    gate = jax.nn.sigmoid(jnp.sum(xef * column[None, :], axis=1))
+    column = lax.dynamic_slice_in_dim(router, expert, 1, axis=1)
+    columns = jnp.concatenate(split3(column), axis=1)
+    gate = jax.nn.sigmoid(jnp.sum(dot(xe, columns, ((1,), (0,))), axis=1))
     coef_row = weight * gate
-    pre = dot(xe, wu, ((1,), (0,)))
-    act = jax.nn.gelu(pre, approximate=False).astype(jnp.bfloat16)
     kind = jnp.arange(2 * n, dtype=jnp.int32)[:, None]
     pair_of = jnp.arange(total, dtype=jnp.int32)[None, :] // height
     member = (kind // 2 == pair_of) & ((kind % 2 == 0) == is_img[None, :])
@@ -476,19 +570,30 @@
     d_high, d_low = split(dvec)
 
     both = dot(jnp.concatenate([d_high, d_low], axis=0), wd, ((1,), (1,)))
-    dhid = (both[: 2 * n] + both[2 * n :]).reshape(n, 2, 1, -1)
-    chosen = jnp.where(is_img.reshape(n, height, 1), dhid[:, 0], dhid[:, 1]).reshape(total, -1)
-    dgl = jnp.sum(act.astype(jnp.float32) * chosen, axis=1) * weight * gate * (1.0 - gate)
-    dpre = (coef_row[:, None] * chosen * gelu_slope(pre)).astype(jnp.bfloat16)
-    back = (dot(dpre, wu, ((1,), (1,))) + dgl[:, None] * column[None, :]).astype(jnp.bfloat16)
-    returned = bring_back(back.reshape(nd, ne, height, D), nd, ne)
-    grad_up = dot(xe, dpre, ((0,), (0,)))[None]
-    grad_down = dot(
+    dhid = both[: 2 * n] + both[2 * n :]
+    h_high, h_low = split(dhid)
+    both = dot(act, jnp.concatenate([h_high, h_low], axis=0), ((1,), (1,)))
+    products = jnp.where(member.T, both[:, : 2 * n] + both[:, 2 * n :], 0.0)
+    dgl = jnp.sum(products, axis=1) * weight * gate * (1.0 - gate)
+    ones = member.T.astype(jnp.bfloat16)
+    chosen = dot(
+        jnp.concatenate([ones, ones], axis=1),
+        jnp.concatenate([h_high, h_low], axis=0),
+        ((1,), (0,)),
+    )
+    dpre = (coef_row[:, None] * chosen * slope).astype(jnp.bfloat16)
+    back = (dot(dpre, wu, ((1,), (1,))) + dgl[:, None] * column[:, 0][None, :]).astype(jnp.bfloat16)
+    returned, grad_up, grad_down = bring_back(
+        back.reshape(nd, ne, height, D),
+        xe,
+        dpre,
         jnp.concatenate([a_high, a_high, a_low], axis=0),
         jnp.concatenate([d_high, d_low, d_high], axis=0),
-        ((0,), (0,)),
-    )[None]
-    router_part = jnp.sum(xef * dgl[:, None], axis=0)
+        nd,
+        ne,
+    )
+    grad_up, grad_down = grad_up[None], grad_down[None]
+    router_part = jnp.sum(dot(jnp.stack(split3(dgl)), xe, ((1,), (0,))), axis=0)
 
     dxn = dot(place, returned.reshape(experts * height, D), ((0,), (0,)))
     gain_part = jnp.sum(dxn * xhat, axis=0)

time: 285 us -> 250 us (0.88)
  matrix products: 46.6 us -> 26.3 us
  local copies, waits for them, and re-layouts: 27.4 us -> 11.6 us
  Pallas kernels: 178 us -> 193 us
  other arithmetic: 25.6 us -> 12.2 us
    dot_general x10 -> x11, matrix products: 44.8 us -> 24.4 us  [dot(): lax.dot_general(a, b, (contract, ((), ())), preferred_element_type=jnp.fl...]
    broadcast_in_dim x4 -> x0, local copies, waits for them, and re-layouts: 17.8 us -> none  [body(): jnp.where(is_img.reshape(n, height, 1), dhid[:, 0], dhid[:, 1])]
    pallas_call x2, Pallas kernels: 136 us -> 151 us  [the longest x1 85.7 us: bring_back(): pl.pallas_call(functools.partial(bring_kernel, nd, ne), out_shape=(jax.Sh...]
    reduce_sum x3 -> x1, other arithmetic: 12.5 us -> 0.14 us  [body(): dgl = jnp.sum(products, axis=1) * weight * gate * (1.0 - gate)]
    unnamed x58 -> x14, local copies, waits for them, and re-layouts: 1.29 us -> 7.5 us
where the time goes in v2:
time: 250 us; the launch traced here: 248 us
  Pallas kernels  193 us (77%)
  matrix products  26.3 us (11%)
  other arithmetic  12.2 us (5%)
  local copies, waits for them, and re-layouts  11.6 us (5%)
  between operations  4.99 us (2%)
    pallas_call x1, Pallas kernels, bring_back(): pl.pallas_call(functools.partial(bring_kernel, nd, ne), out_shape=(jax.Sh...  85.7 us
    pallas_call x1, Pallas kernels, dispatch(): pl.pallas_call(functools.partial(dispatch_kernel, nd, ne), out_shape=(jax...  65 us
    dot_general x11, matrix products, dot(): lax.dot_general(a, b, (contract, ((), ())), preferred_element_type=jnp.fl...  24.4 us
    pallas_call x1, Pallas kernels, everyone(): pl.pallas_call(functools.partial(everyone_kernel, nd, ne), out_shape=jax....  21.8 us
    pallas_call x1, Pallas kernels, pair_sums(): pl.pallas_call(functools.partial(pairs_kernel, nd, ne), out_shape=jax.Sha...  20.9 us
    unnamed x14, local copies, waits for them, and re-layouts  7.5 us

profile of v2, /device:TPU:0, one launch (start us, length us, event | category | flops | bytes accessed | tf_op | source)
XLA Modules:
  0.0 248.4 jit_solution(10184623919467773928)
XLA Ops:
  2.9 0.9 fusion.8
  3.8 0.7 convert_add_fusion
  4.5 1.2 convert_reduce_fusion
  5.7 1.3 multiply_reduce_fusion.2
  7.0 0.1 multiply_reduce_fusion.4
  7.2 0.1 broadcast_in_dim.134
  7.3 0.1 broadcast_in_dim.153
  7.4 0.8 reduce-precision_convert_fusion.7
  8.3 2.4 fusion.5.x_ref
  10.9 0.6 pad_maximum_fusion.6.x_ref
  11.5 65.0 %dispatch.1 = (bf16[4,8,40,1024]{3,2,1,0:T(8,128)(2,1)}, bf16[4,320,1024]{2,1,0:T(8,128)(2,1)}, f32[4,320,1024]{2,1,0:T(8,128)}) custom-call(bf16[8,40,1024]{2,1,0:T(8,128)(2,1)} %fusion.5.x_ref, bf16[1024,1024]{1,0:T(8,128)(2,1)} %bitcast.117), custom_call_target="tpu_custom_call" | custom-call | tf_op jit(solution)/shard_map/dispatch/pallas_call | solution.py:161
  76.5 2.5 %convolution_reduce_fusion = f32[1280]{0:T(1024)S(1)} fusion(bf16[1280,1024]{1,0:T(8,128)(2,1)} %bitcast.107, bf16[1024,1]{0,1:T(2,128)(2,1)S(1)} %get-tuple-element.44, bf16[1024,1]{0,1:T(2,128)(2,1)S(1)} %get-tuple-element.43, bf16[1024,1]{0,1:T(2,128)(2,1)S(1)} %get-tuple-element.25), kind=kOutput, calls=%fused_computation.14 | convolution fusion | flops 7885312 | bytes 2632704 | tf_op jit(solution)/shard_map/dot_general | solution.py:32
  79.1 0.9 fusion.84
  80.1 0.9 slice_convert_fusion
  81.1 0.1 compare_and_fusion
  81.2 0.1 reduce-precision_convert_fusion
  81.4 2.2 fusion.22
  83.7 0.8 pad_maximum_fusion.a_ref
  84.5 0.4 fusion.3
  84.9 0.8 reshape.488.m_ref
  85.7 20.9 %pair_sums.1 = f32[32,8,256]{2,1,0:T(8,128)} custom-call(f32[32,8,256]{2,1,0:T(8,128)} %reshape.488.m_ref, f32[8,256]{1,0:T(8,128)} %pad_maximum_fusion.6.x_ref), custom_call_target="tpu_custom_call" | custom-call | tf_op jit(solution)/shard_map/pair_sums/pallas_call | solution.py:437
  106.6 1.1 reshape.489
  107.7 0.2 fusion.85
  107.9 0.1 fusion.45
  108.1 0.1 fusion.43
  108.2 1.0 fusion.54
  109.8 0.4 multiply_reduce_fusion.6
  110.3 0.1 divide_bitcast_fusion.1
  110.4 0.4 multiply_reduce_fusion.5
  111.0 0.2 copy.20
  111.2 0.2 reshape.491
  111.4 0.8 pad_maximum_fusion.1.d_ref
  112.2 0.8 fusion.1
  113.1 5.1 %fusion.dpre_ref = bf16[1280,1024]{1,0:T(8,128)(2,1)} fusion(f32[4,320,1024]{2,1,0:T(8,128)} %get-tuple-element.14, f32[1280]{0:T(1024)S(1)} %get-tuple-element.40, pred[1280,64]{0,1:T(32,128)(4,1)S(1)} %compare_and_fusion, bf16[64,1024]{1,0:T(8,128)(2,1)S(1)} %get-tuple-element.28, bf16[64,1024]{1,0:T(8,128)(2,1)S(1)} %get-tuple-element.27), kind=kOutput, calls=%fused_computation.1 | convolution fusion | flops 340164608 | bytes 8213504 | tf_op jit(solution)/shard_map/dot_general | solution.py:32
  118.2 1.0 fusion.38
  119.2 0.1 fusion.21
  119.4 0.5 copy-done.1
  119.9 0.5 convolution_reduce_fusion.1
  120.4 6.8 %add_convert_fusion = bf16[1280,1024]{1,0:T(8,128)(2,1)} fusion(bf16[1280,1024]{1,0:T(8,128)(2,1)} %fusion.dpre_ref, f32[1024]{0:T(1024)S(1)} %bitcast.122, f32[1280]{0:T(1024)S(1)} %subtract_multiply_fusion, bf16[1,1024,1024]{2,1,0:T(8,128)(2,1)} %param.14), kind=kOutput, calls=%fused_computation.2 | convolution fusion | flops 2688286720 | bytes 7349248 | tf_op jit(solution)/shard_map/dot_general | solution.py:32
  127.2 85.7 %bring_back.1 = (bf16[8,40,1024]{2,1,0:T(8,128)(2,1)}, f32[1024,1024]{1,0:T(8,128)}, f32[1024,1024]{1,0:T(8,128)}) custom-call(bf16[4,8,40,1024]{3,2,1,0:T(8,128)(2,1)} %bitcast.116, bf16[1280,1024]{1,0:T(8,128)(2,1)} %bitcast.110, bf16[1280,1024]{1,0:T(8,128)(2,1)} %fusion.dpre_ref, bf16[192,1024]{1,0:T(8,128)(2,1)} %pad_maximum_fusion.a_ref, ...), custom_call_target="tpu_custom_call" | custom-call | tf_op jit(solution)/shard_map/bring_back/pallas_call | solution.py:365
  212.9 1.8 multiply_reduce_fusion
  214.7 0.6 pad_maximum_fusion.7.x_ref
  215.3 1.2 fusion.18
  216.5 21.8 %everyone.1 = f32[32,8,256]{2,1,0:T(8,128)} custom-call(f32[8,256]{1,0:T(8,128)} %pad_maximum_fusion.7.x_ref), custom_call_target="tpu_custom_call" | custom-call | tf_op jit(solution)/shard_map/everyone/pallas_call | solution.py:465
  238.4 1.1 reshape.496
  239.5 0.9 slice_reduce_fusion.1
  240.3 4.9 %copy.60 = f32[1,1024,1024]{2,1,0:T(8,128)} copy(f32[1,1024,1024]{2,1,0:T(8,128)} %bitcast.115) | data formatting | bytes 8388608
  245.3 2.0 copy.61
  (55 shorter events, 1.1 us)
Async XLA Ops:
  0.6 83.8 %copy-start = (bf16[1,1024,1024]{2,1,0:T(8,128)(2,1)S(1)}, bf16[1,1024,1024]{2,1,0:T(8,128)(2,1)}, u32[]{:S(2)}) copy-start(bf16[1,1024,1024]{2,1,0:T(8,128)(2,1)} %param.15) | copy-start | bytes 6291460
  0.6 10.0 %copy-start.3 = (bf16[1,212,1024]{2,1,0:T(8,128)(2,1)S(1)}, bf16[1,212,1024]{2,1,0:T(8,128)(2,1)}, u32[]{:S(2)}) copy-start(bf16[1,212,1024]{2,1,0:T(8,128)(2,1)} %param.9) | copy-start | bytes 1302532
  113.1 5.1 %copy-start.2 = (bf16[4,320,1024]{2,1,0:T(8,128)(2,1)S(1)}, bf16[4,320,1024]{2,1,0:T(8,128)(2,1)}, u32[]{:S(2)}) copy-start(bf16[4,320,1024]{2,1,0:T(8,128)(2,1)} %get-tuple-element.13) | copy-start | bytes 7864324
  118.2 1.7 copy-start.1
  127.2 85.7 %copy-start.5 = (f32[1024]{0:T(1024)S(1)}, f32[1024]{0:T(1024)}, u32[]{:S(2)}) copy-start(f32[1024]{0:T(1024)} %param.12) | copy-start | bytes 12292
  240.3 4.9 %copy-start.4 = (f32[1024,1024]{1,0:T(8,128)S(1)}, f32[1024,1024]{1,0:T(8,128)}, u32[]{:S(2)}) copy-start(f32[1024,1024]{1,0:T(8,128)} %get-tuple-element.17) | copy-start | bytes 12582916

commit v3 on v2

--- a/solution.py
+++ b/solution.py
@@ -182,27 +182,52 @@
 def bring_kernel(
     nd,
     ne,
-    b_ref,
     x_ref,
-    dpre_ref,
+    slope_ref,
+    w_ref,
+    q_ref,
+    h_ref,
+    c_ref,
     a_ref,
     d_ref,
+    rp_ref,
     ret_ref,
     gup_ref,
     gdn_ref,
+    rall_ref,
+    b_ref,
+    dpre_ref,
     from_dn,
     from_up,
-    fin,
     up_sem,
     dn_sem,
     ru_sem,
     rd_sem,
     a_sem,
     ra_sem,
+    rs_sem,
+    rr_sem,
 ):
+    _, _, height, width = b_ref.shape
+    plane = ne * height
     window = min(4, ne)
+    lag = min(4, ne)
     z = lax.axis_index("dp")
     e = lax.axis_index("expert")
+    me = z * ne + e
+    rall_ref[me] = rp_ref[...]
+    router_arrive, router_drain = spread(nd, ne, me, lambda t: rp_ref, rall_ref, rs_sem, rr_sem)
+
+    def produce(o):
+        part = pl.ds(o * plane, plane)
+        dact = jnp.dot(q_ref[part, :], h_ref[o], preferred_element_type=jnp.float32)
+        dpre = (dact * slope_ref[part, :]).astype(jnp.bfloat16)
+        dpre_ref[part, :] = dpre
+        back = lax.dot_general(
+            dpre, w_ref[...], (((1,), (1,)), ((), ())), preferred_element_type=jnp.float32
+        )
+        back += jnp.dot(q_ref[part, :], c_ref[...], preferred_element_type=jnp.float32)
+        b_ref[o] = back.astype(jnp.bfloat16).reshape(ne, height, width)
 
     def rise(src, o, s):
         return pltpu.make_async_remote_copy(
@@ -226,7 +251,7 @@
 
     def cross(s):
         return pltpu.make_async_remote_copy(
-            src_ref=fin.at[s],
+            src_ref=b_ref.at[z, s],
             dst_ref=ret_ref.at[e],
             send_sem=a_sem.at[s],
             recv_sem=ra_sem.at[e],
@@ -236,7 +261,7 @@
 
     def back(s):
         return pltpu.make_async_remote_copy(
-            src_ref=fin.at[s],
+            src_ref=b_ref.at[z, s],
             dst_ref=ret_ref.at[s],
             send_sem=a_sem.at[s],
             recv_sem=ra_sem.at[s],
@@ -267,69 +292,84 @@
                 preferred_element_type=jnp.float32,
             )
 
-    def add(held, o, s):
-        total = held[o, s].astype(jnp.float32) + b_ref[o, s].astype(jnp.float32)
+    def add(held, other, o, s):
+        total = held[o, s].astype(jnp.float32) + other[o, s].astype(jnp.float32)
         held[o, s] = total.astype(held.dtype)
 
+    upper = (z >= nd // 2).astype(jnp.int32)
+
+    def travel(step):
+        t_up = step - lag * upper
+        t_dn = step - lag * (1 - upper)
+
+        @pl.when((t_up >= 0) & (t_up < (nd - 1 - z) * ne))
+        def _():
+            o = nd - 1 - t_up // ne
+            s = place(t_up)
+
+            @pl.when(t_up >= window)
+            def _():
+                risen(t_up - window)
+
+            @pl.when(z == 0)
+            def _():
+                rise(b_ref, o, s).start()
+
+            @pl.when(z > 0)
+            def _():
+                rise(from_dn, o, s).wait_recv()
+                add(from_dn, b_ref, o, s)
+                rise(from_dn, o, s).start()
+
+        @pl.when((t_dn >= 0) & (t_dn < z * ne))
+        def _():
+            o = t_dn // ne
+            s = place(t_dn)
+
+            @pl.when(t_dn >= window)
+            def _():
+                fallen(t_dn - window)
+
+            @pl.when(z == nd - 1)
+            def _():
+                fall(b_ref, o, s).start()
+
+            @pl.when(z < nd - 1)
+            def _():
+                fall(from_up, o, s).wait_recv()
+                add(from_up, b_ref, o, s)
+                fall(from_up, o, s).start()
+
     for j in range(nd - 1):
-        high, low = nd - 1 - j, j
+        if j <= nd - 1 - j:
+            produce(nd - 1 - j)
+        if j < nd - 1 - j:
+            produce(j)
 
         @pl.loop(0, ne)
         def _(k):
-            s = lax.rem(e + k + 1, ne)
-            t = j * ne + k
-
-            @pl.when((high > z) & (t >= window))
-            def _():
-                risen(t - window)
-
-            @pl.when((low < z) & (t >= window))
-            def _():
-                fallen(t - window)
-
-            @pl.when((high > z) & (z == 0))
-            def _():
-                rise(b_ref, high, s).start()
-
-            @pl.when((high > z) & (z > 0))
-            def _():
-                rise(from_dn, high, s).wait_recv()
-                add(from_dn, high, s)
-                rise(from_dn, high, s).start()
-
-            @pl.when((low < z) & (z == nd - 1))
-            def _():
-                fall(b_ref, low, s).start()
-
-            @pl.when((low < z) & (z < nd - 1))
-            def _():
-                fall(from_up, low, s).wait_recv()
-                add(from_up, low, s)
-                fall(from_up, low, s).start()
-
-            if j == 0:
+            travel(j * ne + k)
+            if j == min(nd // 2, nd - 2):
                 weights(x_ref, dpre_ref, gup_ref, k)
-            if j == min(1, nd - 2):
                 weights(a_ref, d_ref, gdn_ref, k)
 
+    @pl.loop((nd - 1) * ne, (nd - 1) * ne + lag)
+    def _(step):
+        travel(step)
+
     @pl.loop(0, ne)
     def _(k):
         s = lax.rem(e + k + 1, ne)
-        fin[s] = b_ref[z, s]
 
         @pl.when(z > 0)
         def _():
             rise(from_dn, z, s).wait_recv()
-            fin[s] = (fin[s].astype(jnp.float32) + from_dn[z, s].astype(jnp.float32)).astype(
-                fin.dtype
-            )
+            add(b_ref, from_dn, z, s)
 
         @pl.when(z < nd - 1)
         def _():
             fall(from_up, z, s).wait_recv()
-            fin[s] = (fin[s].astype(jnp.float32) + from_up[z, s].astype(jnp.float32)).astype(
-                fin.dtype
-            )
+            add(b_ref, from_up, z, s)
 
         @pl.when(s != e)
         def _():
@@ -337,7 +377,7 @@
 
         @pl.when(s == e)
         def _():
-            ret_ref[e] = fin[e]
+            ret_ref[e] = b_ref[z, e]
 
     @pl.loop(1, ne)
     def _(k):
@@ -357,34 +397,43 @@
         def _():
             fallen(z * ne - window + i)
 
-
-def bring_back(partial_rows, xe, dpre, a, d, nd, ne):
-    _, _, height, width = partial_rows.shape
-    dtype = partial_rows.dtype
+    router_arrive()
+    router_drain()
+
+def bring_back(xe, slope, weights, q, h, c, a, d, router_part, nd, ne):
+    total, width = xe.shape
+    hidden = slope.shape[1]
+    n = nd * ne
+    height = total // n
+    dtype = jnp.bfloat16
     dma = pltpu.SemaphoreType.DMA
     return pl.pallas_call(
         functools.partial(bring_kernel, nd, ne),
         out_shape=(
             jax.ShapeDtypeStruct((ne, height, width), dtype),
-            jax.ShapeDtypeStruct((xe.shape[1], dpre.shape[1]), jnp.float32),
-            jax.ShapeDtypeStruct((a.shape[1], d.shape[1]), jnp.float32),
+            jax.ShapeDtypeStruct((width, hidden), jnp.float32),
+            jax.ShapeDtypeStruct((hidden, width), jnp.float32),
+            jax.ShapeDtypeStruct((n,) + router_part.shape, jnp.float32),
         ),
-        in_specs=[vmem()] * 5,
-        out_specs=(vmem(), vmem(), vmem()),
+        in_specs=[vmem()] * 9,
+        out_specs=(vmem(),) * 4,
         scratch_shapes=[
             pltpu.VMEM((nd, ne, height, width), dtype),
+            pltpu.VMEM((total, hidden), dtype),
             pltpu.VMEM((nd, ne, height, width), dtype),
-            pltpu.VMEM((ne, height, width), dtype),
+            pltpu.VMEM((nd, ne, height, width), dtype),
             dma((nd, ne)),
             dma((nd, ne)),
             dma((nd, ne)),
             dma((nd, ne)),
             dma((ne,)),
             dma((ne,)),
+            dma((n,)),
+            dma((n,)),
         ],
         compiler_params=pltpu.CompilerParams(has_side_effects=True),
         name="bring_back",
-    )(partial_rows, xe, dpre, a, d)
+    )(xe, slope, weights, q, h, c, a, d, router_part)
 
 
 def spread(nd, ne, me, src, dst, send_sem, recv_sem):
@@ -404,31 +453,32 @@
     def _(k):
         copy(lax.rem(me + k, n), me).start()
 
-    @pl.loop(1, n)
-    def _(k):
-        t = lax.rem(me + n - k, n)
-        copy(t, t).wait_recv()
-
-    return copy
-
-
-def drain(n, me, copy):
-    @pl.loop(1, n)
-    def _(k):
-        copy(lax.rem(me + k, n), me).wait_send()
+    def arrive():
+        @pl.loop(1, n)
+        def _(k):
+            t = lax.rem(me + n - k, n)
+            copy(t, t).wait_recv()
+
+    def drain():
+        @pl.loop(1, n)
+        def _(k):
+            copy(lax.rem(me + k, n), me).wait_send()
+
+    return arrive, drain
 
 
 def pairs_kernel(nd, ne, m_ref, x_ref, out_ref, held, own, s1, r1, s2, r2):
-    n = nd * ne
     me = lax.axis_index("dp") * ne + lax.axis_index("expert")
     held[me] = m_ref[me]
-    first = spread(nd, ne, me, lambda t: m_ref.at[t], held, s1, r1)
+    arrive, drain_first = spread(nd, ne, me, lambda t: m_ref.at[t], held, s1, r1)
+    arrive()
     total = jnp.sum(held[...], axis=0) + x_ref[...]
     own[...] = total
     out_ref[me] = total
-    second = spread(nd, ne, me, lambda t: own, out_ref, s2, r2)
-    drain(n, me, first)
-    drain(n, me, second)
+    arrive, drain_second = spread(nd, ne, me, lambda t: own, out_ref, s2, r2)
+    arrive()
+    drain_first()
+    drain_second()
 
 
 def pair_sums(m, x, nd, ne):
@@ -453,10 +503,11 @@
 
 
 def everyone_kernel(nd, ne, x_ref, out_ref, s1, r1):
-    n = nd * ne
     me = lax.axis_index("dp") * ne + lax.axis_index("expert")
     out_ref[me] = x_ref[...]
-    drain(n, me, spread(nd, ne, me, lambda t: x_ref, out_ref, s1, r1))
+    arrive, drain = spread(nd, ne, me, lambda t: x_ref, out_ref, s1, r1)
+    arrive()
+    drain()
 
 
 def everyone(x, nd, ne):
@@ -575,25 +626,28 @@
     both = dot(act, jnp.concatenate([h_high, h_low], axis=0), ((1,), (1,)))
     products = jnp.where(member.T, both[:, : 2 * n] + both[:, 2 * n :], 0.0)
     dgl = jnp.sum(products, axis=1) * weight * gate * (1.0 - gate)
-    ones = member.T.astype(jnp.bfloat16)
-    chosen = dot(
-        jnp.concatenate([ones, ones], axis=1),
-        jnp.concatenate([h_high, h_low], axis=0),
-        ((1,), (0,)),
-    )
-    dpre = (coef_row[:, None] * chosen * slope).astype(jnp.bfloat16)
-    back = (dot(dpre, wu, ((1,), (1,))) + dgl[:, None] * column[:, 0][None, :]).astype(jnp.bfloat16)
-    returned, grad_up, grad_down = bring_back(
-        back.reshape(nd, ne, height, D),
+    router_part = jnp.sum(dot(jnp.stack(split3(dgl)), xe, ((1,), (0,))), axis=0)
+    local = jnp.arange(2 * ne, dtype=jnp.int32)[None, :]
+    pair_in_plane = lax.rem(jnp.arange(total, dtype=jnp.int32)[:, None] // height, ne)
+    own = (local // 2 == pair_in_plane) & ((local % 2 == 0) == is_img[:, None])
+    qt_high, qt_low = split(jnp.where(own, coef_row[:, None], 0.0))
+    h_high, h_low = h_high.reshape(nd, 2 * ne, -1), h_low.reshape(nd, 2 * ne, -1)
+    g_high, g_low = split(dgl[:, None])
+    c_high, c_low = split(column.T)
+    returned, grad_up, grad_down, router_all = bring_back(
         xe,
-        dpre,
+        slope,
+        wu,
+        jnp.concatenate([qt_high, qt_high, qt_low, g_high, g_high, g_low], axis=1),
+        jnp.pad(jnp.concatenate([h_high, h_low, h_high], axis=1), ((0, 0), (0, 3), (0, 0))),
+        jnp.pad(jnp.concatenate([c_high, c_low, c_high], axis=0), ((6 * ne, 0), (0, 0))),
         jnp.concatenate([a_high, a_high, a_low], axis=0),
         jnp.concatenate([d_high, d_low, d_high], axis=0),
+        router_part.reshape(8, D // 8),
         nd,
         ne,
     )
     grad_up, grad_down = grad_up[None], grad_down[None]
-    router_part = jnp.sum(dot(jnp.stack(split3(dgl)), xe, ((1,), (0,))), axis=0)
 
     dxn = dot(place, returned.reshape(experts * height, D), ((0,), (0,)))
     gain_part = jnp.sum(dxn * xhat, axis=0)
@@ -608,10 +662,8 @@
         jnp.where(mark > 0.0, 1.0 / length[0], 0.0)[:, None] * mine[1:2],
     )
     grad_tokens = (dy + normed).astype(jnp.bfloat16).reshape(1, SEQ, D)
-    last = everyone(jnp.concatenate([gain_part, router_part]).reshape(8, 2 * D // 8), nd, ne)
-    last = last.reshape(nd, ne, 2, D)
-    gain_grad = jnp.sum(last[:, :, 0], axis=(0, 1))
-    grad_router = jnp.sum(last[:, :, 1], axis=0).T
+    gain_grad = jnp.sum(everyone(gain_part.reshape(8, D // 8), nd, ne), axis=0).reshape(D)
+    grad_router = jnp.sum(router_all.reshape(nd, ne, D), axis=0).T
     return (loss.reshape(1), grad_tokens, grad_up, grad_down, grad_router, gain_grad)
 
 

time: 250 us -> 214 us (0.86)
  Pallas kernels: 193 us -> 166 us
  matrix products: 26.3 us -> 15.6 us
    pallas_call x1, Pallas kernels: 85.7 us -> 64.5 us  [bring_back(): pl.pallas_call(functools.partial(bring_kernel, nd, ne), out_shape=(jax.Sh...]
    dot_general x11 -> x9, matrix products: 24.4 us -> 13.7 us  [dot(): lax.dot_general(a, b, (contract, ((), ())), preferred_element_type=jnp.fl...]
    pallas_call x1, Pallas kernels: 21.8 us -> 15.5 us  [everyone(): pl.pallas_call(functools.partial(everyone_kernel, nd, ne), out_shape=jax....]
where the time goes in v3:
time: 214 us; the launch traced here: 213 us
  Pallas kernels  166 us (78%)
  matrix products  15.6 us (7%)
  local copies, waits for them, and re-layouts  13.5 us (6%)
  other arithmetic  13.4 us (6%)
  between operations  5 us (2%)
    pallas_call x1, Pallas kernels, dispatch(): pl.pallas_call(functools.partial(dispatch_kernel, nd, ne), out_shape=(jax...  65 us
    pallas_call x1, Pallas kernels, bring_back(): pl.pallas_call(functools.partial(bring_kernel, nd, ne), out_shape=(jax.Sh...  64.5 us
    pallas_call x1, Pallas kernels, pair_sums(): pl.pallas_call(functools.partial(pairs_kernel, nd, ne), out_shape=jax.Sha...  20.9 us
    pallas_call x1, Pallas kernels, everyone(): pl.pallas_call(functools.partial(everyone_kernel, nd, ne), out_shape=jax....  15.5 us
    dot_general x9, matrix products, dot(): lax.dot_general(a, b, (contract, ((), ())), preferred_element_type=jnp.fl...  13.7 us
    unnamed x14, local copies, waits for them, and re-layouts  7.59 us

profile of v3, /device:TPU:0, one launch (start us, length us, event | category | flops | bytes accessed | tf_op | source)
XLA Modules:
  0.0 213.3 jit_solution(18015169126148300542)
XLA Ops:
  2.9 0.9 fusion.7
  3.8 0.7 convert_add_fusion
  4.5 1.2 convert_reduce_fusion
  5.7 1.3 multiply_reduce_fusion.2
  7.0 0.1 multiply_reduce_fusion.4
  7.2 0.1 broadcast_in_dim.157
  7.6 0.8 fusion.84
  8.4 0.8 reduce-precision_convert_fusion.10
  9.2 0.7 fusion.58.c_ref
  9.8 2.4 %fusion.4.x_ref = bf16[8,40,1024]{2,1,0:T(8,128)(2,1)} fusion(bf16[8,1024]{1,0:T(8,128)(2,1)S(1)} %pad_bitcast_fusion, pred[40]{0:T(512)(128)(4,1)S(1)} %iota_compare_fusion.10, bf16[1,212,1024]{2,1,0:T(8,128)(2,1)} %param.9, f32[1024]{0:T(1024)} %param.12, f32[212]{0:T(256)S(1)} %add_rsqrt_fusion, f32[212]{0:T(256)S(1)} %broadcast_multiply_fusion.3, ...), kind=kOutput, calls=%fused_computation.5 | convolution fusion | flops 140417280 | bytes 1113880 | tf_op jit(solution)/shard_map/dot_general | solution.py:32
  12.5 0.6 pad_maximum_fusion.3.x_ref
  13.1 65.0 %dispatch.1 = (bf16[4,8,40,1024]{3,2,1,0:T(8,128)(2,1)}, bf16[4,320,1024]{2,1,0:T(8,128)(2,1)}, f32[4,320,1024]{2,1,0:T(8,128)}) custom-call(bf16[8,40,1024]{2,1,0:T(8,128)(2,1)} %fusion.4.x_ref, bf16[1024,1024]{1,0:T(8,128)(2,1)} %bitcast.118), custom_call_target="tpu_custom_call" | custom-call | tf_op jit(solution)/shard_map/dispatch/pallas_call | solution.py:161
  78.1 2.5 %convolution_reduce_fusion = f32[1280]{0:T(1024)S(1)} fusion(bf16[1280,1024]{1,0:T(8,128)(2,1)} %bitcast.112, bf16[1024,1]{0,1:T(2,128)(2,1)S(1)} %get-tuple-element.41, bf16[1024,1]{0,1:T(2,128)(2,1)S(1)} %get-tuple-element.40, bf16[1024,1]{0,1:T(2,128)(2,1)S(1)} %get-tuple-element.39), kind=kOutput, calls=%fused_computation.11 | convolution fusion | flops 7885312 | bytes 2632704 | tf_op jit(solution)/shard_map/dot_general | solution.py:32
  80.7 0.9 slice.65
  81.9 0.1 reduce-precision_convert_fusion
  82.1 2.2 %fusion.23 = f32[128,1024]{1,0:T(8,128)S(1)} fusion(bf16[1280,1024]{1,0:T(8,128)(2,1)} %bitcast.116, bf16[64,1280]{1,0:T(8,128)(2,1)S(1)} %get-tuple-element.45, bf16[64,1280]{1,0:T(8,128)(2,1)S(1)} %get-tuple-element.44), kind=kOutput, calls=%fused_computation.50 | convolution fusion | flops 336199680 | bytes 3473408 | tf_op jit(solution)/shard_map/dot_general | solution.py:32
  84.4 0.8 pad_maximum_fusion.a_ref
  85.2 0.4 fusion.2
  85.7 0.8 reshape.709.m_ref
  86.4 20.9 %pair_sums.1 = f32[32,8,256]{2,1,0:T(8,128)} custom-call(f32[32,8,256]{2,1,0:T(8,128)} %reshape.709.m_ref, f32[8,256]{1,0:T(8,128)} %pad_maximum_fusion.3.x_ref), custom_call_target="tpu_custom_call" | custom-call | tf_op jit(solution)/shard_map/pair_sums/pallas_call | solution.py:487
  107.4 1.1 reshape.710
  108.5 0.2 fusion.95
  108.7 0.1 fusion.52
  108.8 0.1 fusion.50
  109.0 1.0 fusion.64
  110.6 0.4 multiply_reduce_fusion.6
  111.0 0.1 divide_bitcast_fusion.1
  111.1 0.4 multiply_reduce_fusion.5
  111.7 0.2 copy.36
  111.9 0.2 reshape.712
  112.2 0.8 pad_maximum_fusion.1.d_ref
  113.0 0.8 fusion
  113.9 0.1 copy-done.2
  114.0 1.0 fusion.39
  115.0 0.1 fusion.22
  115.3 0.5 copy-done.1
  115.8 1.1 convolution_reduce_fusion.1
  116.9 0.9 copy.37.q_ref
  117.8 0.8 fusion.13.h_ref
  118.6 64.5 %bring_back.1 = (bf16[8,40,1024]{2,1,0:T(8,128)(2,1)}, f32[1024,1024]{1,0:T(8,128)}, f32[1024,1024]{1,0:T(8,128)}, f32[32,8,128]{2,1,0:T(8,128)}) custom-call(bf16[1280,1024]{1,0:T(8,128)(2,1)} %bitcast.114, f32[1280,1024]{1,0:T(8,128)} %bitcast.120, bf16[1024,1024]{1,0:T(8,128)(2,1)} %bitcast.119, bf16[1280,51]{1,0:T(8,128)(2,1)} %copy.37.q_ref, ...), custom_call_target="tpu_custom_call" | custom-call | tf_op jit(solution)/shard_map/bring_back/pallas_call | solution.py:410
  183.1 0.9 reshape.719
  184.0 0.6 reduce_sum.193
  184.7 2.4 %multiply_reduce_fusion = (f32[1024]{0:T(1024)}, f32[212]{0:T(256)S(1)}, f32[212]{0:T(256)S(1)}, f32[212,1024]{1,0:T(8,128)S(1)}) fusion(bf16[1,212,1024]{2,1,0:T(8,128)(2,1)S(1)} %copy-done.3, f32[212]{0:T(256)S(1)} %add_rsqrt_fusion, f32[212]{0:T(256)S(1)} %broadcast_multiply_fusion.3, f32[1024]{0:T(1024)S(1)} %copy-done.5, ...), kind=kOutput, calls=%fused_computation.20 | convolution fusion | flops 140956512 | bytes 1970320 | tf_op jit(solution)/shard_map/dot_general | solution.py:32
  187.0 1.2 fusion.19
  188.2 15.5 %everyone.1 = f32[32,8,128]{2,1,0:T(8,128)} custom-call(f32[8,128]{1,0:T(8,128)} %bitcast.130), custom_call_target="tpu_custom_call" | custom-call | tf_op jit(solution)/shard_map/everyone/pallas_call | solution.py:516
  203.7 1.5 reduce_sum.195
  205.2 4.9 %copy.77 = f32[1,1024,1024]{2,1,0:T(8,128)} copy(f32[1,1024,1024]{2,1,0:T(8,128)} %bitcast.122) | data formatting | bytes 8388608
  210.2 2.0 copy.78
  (61 shorter events, 1.5 us)
Async XLA Ops:
  0.6 84.6 %copy-start = (bf16[1,1024,1024]{2,1,0:T(8,128)(2,1)S(1)}, bf16[1,1024,1024]{2,1,0:T(8,128)(2,1)}, u32[]{:S(2)}) copy-start(bf16[1,1024,1024]{2,1,0:T(8,128)(2,1)} %param.15) | copy-start | bytes 6291460
  0.6 11.5 %copy-start.3 = (bf16[1,212,1024]{2,1,0:T(8,128)(2,1)S(1)}, bf16[1,212,1024]{2,1,0:T(8,128)(2,1)}, u32[]{:S(2)}) copy-start(bf16[1,212,1024]{2,1,0:T(8,128)(2,1)} %param.9) | copy-start | bytes 1302532
  112.1 1.9 copy-start.2
  114.0 1.7 copy-start.1
  118.6 66.1 %copy-start.5 = (f32[1024]{0:T(1024)S(1)}, f32[1024]{0:T(1024)}, u32[]{:S(2)}) copy-start(f32[1024]{0:T(1024)} %param.12) | copy-start | bytes 12292
  205.2 4.9 %copy-start.4 = (f32[1024,1024]{1,0:T(8,128)S(1)}, f32[1024,1024]{1,0:T(8,128)}, u32[]{:S(2)}) copy-start(f32[1024,1024]{1,0:T(8,128)} %get-tuple-element.18) | copy-start | bytes 12582916

commit v4 on v3

--- a/solution.py
+++ b/solution.py
@@ -502,23 +502,72 @@
     )(m, x)
 
 
-def everyone_kernel(nd, ne, x_ref, out_ref, s1, r1):
-    me = lax.axis_index("dp") * ne + lax.axis_index("expert")
-    out_ref[me] = x_ref[...]
-    arrive, drain = spread(nd, ne, me, lambda t: x_ref, out_ref, s1, r1)
-    arrive()
-    drain()
+def everyone_kernel(nd, ne, x_ref, out_ref, held, own, planes, s1, r1, s2, r2):
+    z = lax.axis_index("dp")
+    e = lax.axis_index("expert")
+
+    def across(t, sender):
+        return pltpu.make_async_remote_copy(
+            src_ref=x_ref,
+            dst_ref=held.at[sender],
+            send_sem=s1.at[t],
+            recv_sem=r1.at[sender],
+            device_id=(z, t),
+            device_id_type=MESH,
+        )
+
+    def along(t, sender):
+        return pltpu.make_async_remote_copy(
+            src_ref=own,
+            dst_ref=planes.at[sender],
+            send_sem=s2.at[t],
+            recv_sem=r2.at[sender],
+            device_id=(t, e),
+            device_id_type=MESH,
+        )
+
+    def exchange(count, here, copy):
+        @pl.loop(1, count)
+        def _(k):
+            copy(lax.rem(here + k, count), here).start()
+
+        @pl.loop(1, count)
+        def _(k):
+            t = lax.rem(here + count - k, count)
+            copy(t, t).wait_recv()
+
+    def drain(count, here, copy):
+        @pl.loop(1, count)
+        def _(k):
+            copy(lax.rem(here + k, count), here).wait_send()
+
+    held[e] = x_ref[...]
+    exchange(ne, e, across)
+    total = jnp.sum(held[...], axis=0)
+    own[...] = total
+    planes[z] = total
+    exchange(nd, z, along)
+    out_ref[...] = jnp.sum(planes[...], axis=0)
+    drain(ne, e, across)
+    drain(nd, z, along)
 
 
 def everyone(x, nd, ne):
-    n = nd * ne
     dma = pltpu.SemaphoreType.DMA
     return pl.pallas_call(
         functools.partial(everyone_kernel, nd, ne),
-        out_shape=jax.ShapeDtypeStruct((n,) + x.shape, x.dtype),
+        out_shape=jax.ShapeDtypeStruct(x.shape, x.dtype),
         in_specs=[vmem()],
         out_specs=vmem(),
-        scratch_shapes=[dma((n,)), dma((n,))],
+        scratch_shapes=[
+            pltpu.VMEM((ne,) + x.shape, x.dtype),
+            pltpu.VMEM(x.shape, x.dtype),
+            pltpu.VMEM((nd,) + x.shape, x.dtype),
+            dma((ne,)),
+            dma((ne,)),
+            dma((nd,)),
+            dma((nd,)),
+        ],
         compiler_params=pltpu.CompilerParams(has_side_effects=True),
         name="everyone",
     )(x)
@@ -662,7 +711,7 @@
         jnp.where(mark > 0.0, 1.0 / length[0], 0.0)[:, None] * mine[1:2],
     )
     grad_tokens = (dy + normed).astype(jnp.bfloat16).reshape(1, SEQ, D)
-    gain_grad = jnp.sum(everyone(gain_part.reshape(8, D // 8), nd, ne), axis=0).reshape(D)
+    gain_grad = everyone(gain_part.reshape(8, D // 8), nd, ne).reshape(D)
     grad_router = jnp.sum(router_all.reshape(nd, ne, D), axis=0).T
     return (loss.reshape(1), grad_tokens, grad_up, grad_down, grad_router, gain_grad)
 

time: 214 us -> 214 us (level)
    unnamed x14 -> x17, local copies, waits for them, and re-layouts: 7.59 us -> 8.19 us
where the time goes in v4:
time: 214 us
  Pallas kernels  167 us (78%)
  matrix products  15.6 us (7%)
  local copies, waits for them, and re-layouts  14.1 us (7%)
  other arithmetic  11.8 us (6%)
  between operations  5.01 us (2%)
    pallas_call x1, Pallas kernels, dispatch(): pl.pallas_call(functools.partial(dispatch_kernel, nd, ne), out_shape=(jax...  65 us
    pallas_call x1, Pallas kernels, bring_back(): pl.pallas_call(functools.partial(bring_kernel, nd, ne), out_shape=(jax.Sh...  64.5 us
    pallas_call x1, Pallas kernels, pair_sums(): pl.pallas_call(functools.partial(pairs_kernel, nd, ne), out_shape=jax.Sha...  20.9 us
    pallas_call x1, Pallas kernels, everyone(): pl.pallas_call(functools.partial(everyone_kernel, nd, ne), out_shape=jax....  16.6 us
    dot_general x9, matrix products, dot(): lax.dot_general(a, b, (contract, ((), ())), preferred_element_type=jnp.fl...  13.7 us
    unnamed x17, local copies, waits for them, and re-layouts  8.19 us

profile of v4, /device:TPU:0, one launch (start us, length us, event | category | flops | bytes accessed | tf_op | source)
XLA Modules:
  0.0 213.5 jit_solution(14898223606427165511)
XLA Ops:
  2.9 0.9 fusion.7
  3.8 0.7 convert_add_fusion
  4.5 1.2 convert_reduce_fusion
  5.7 1.3 multiply_reduce_fusion.2
  7.0 0.1 multiply_reduce_fusion.4
  7.2 0.1 broadcast_in_dim.157
  7.6 0.8 fusion.84
  8.4 0.8 reduce-precision_convert_fusion.10
  9.2 0.7 fusion.58.c_ref
  9.8 2.4 %fusion.4.x_ref = bf16[8,40,1024]{2,1,0:T(8,128)(2,1)} fusion(bf16[8,1024]{1,0:T(8,128)(2,1)S(1)} %pad_bitcast_fusion, pred[40]{0:T(512)(128)(4,1)S(1)} %iota_compare_fusion.10, bf16[1,212,1024]{2,1,0:T(8,128)(2,1)} %param.9, f32[1024]{0:T(1024)} %param.12, f32[212]{0:T(256)S(1)} %add_rsqrt_fusion, f32[212]{0:T(256)S(1)} %broadcast_multiply_fusion.3, ...), kind=kOutput, calls=%fused_computation.5 | convolution fusion | flops 140417280 | bytes 1113880 | tf_op jit(solution)/shard_map/dot_general | solution.py:32
  12.5 0.6 pad_maximum_fusion.3.x_ref
  13.1 65.0 %dispatch.1 = (bf16[4,8,40,1024]{3,2,1,0:T(8,128)(2,1)}, bf16[4,320,1024]{2,1,0:T(8,128)(2,1)}, f32[4,320,1024]{2,1,0:T(8,128)}) custom-call(bf16[8,40,1024]{2,1,0:T(8,128)(2,1)} %fusion.4.x_ref, bf16[1024,1024]{1,0:T(8,128)(2,1)} %bitcast.118), custom_call_target="tpu_custom_call" | custom-call | tf_op jit(solution)/shard_map/dispatch/pallas_call | solution.py:161
  78.1 2.5 %convolution_reduce_fusion = f32[1280]{0:T(1024)S(1)} fusion(bf16[1280,1024]{1,0:T(8,128)(2,1)} %bitcast.112, bf16[1024,1]{0,1:T(2,128)(2,1)S(1)} %get-tuple-element.41, bf16[1024,1]{0,1:T(2,128)(2,1)S(1)} %get-tuple-element.40, bf16[1024,1]{0,1:T(2,128)(2,1)S(1)} %get-tuple-element.39), kind=kOutput, calls=%fused_computation.11 | convolution fusion | flops 7885312 | bytes 2632704 | tf_op jit(solution)/shard_map/dot_general | solution.py:32
  80.7 0.9 slice.65
  81.9 0.1 reduce-precision_convert_fusion
  82.1 2.2 %fusion.23 = f32[128,1024]{1,0:T(8,128)S(1)} fusion(bf16[1280,1024]{1,0:T(8,128)(2,1)} %bitcast.116, bf16[64,1280]{1,0:T(8,128)(2,1)S(1)} %get-tuple-element.45, bf16[64,1280]{1,0:T(8,128)(2,1)S(1)} %get-tuple-element.44), kind=kOutput, calls=%fused_computation.50 | convolution fusion | flops 336199680 | bytes 3473408 | tf_op jit(solution)/shard_map/dot_general | solution.py:32
  84.4 0.8 pad_maximum_fusion.a_ref
  85.2 0.4 fusion.2
  85.7 0.8 reshape.709.m_ref
  86.4 20.9 %pair_sums.1 = f32[32,8,256]{2,1,0:T(8,128)} custom-call(f32[32,8,256]{2,1,0:T(8,128)} %reshape.709.m_ref, f32[8,256]{1,0:T(8,128)} %pad_maximum_fusion.3.x_ref), custom_call_target="tpu_custom_call" | custom-call | tf_op jit(solution)/shard_map/pair_sums/pallas_call | solution.py:487
  107.4 1.1 reshape.710
  108.5 0.2 fusion.95
  108.7 0.1 fusion.52
  108.8 0.1 fusion.50
  109.0 1.0 fusion.64
  110.6 0.4 multiply_reduce_fusion.6
  111.0 0.1 divide_bitcast_fusion.1
  111.1 0.4 multiply_reduce_fusion.5
  111.7 0.2 copy.36
  111.9 0.2 reshape.712
  112.2 0.8 pad_maximum_fusion.1.d_ref
  113.0 0.8 fusion
  113.9 0.1 copy-done.2
  114.0 1.0 fusion.39
  115.0 0.1 fusion.22
  115.3 0.5 copy-done.1
  115.7 1.1 convolution_reduce_fusion.1
  116.9 0.9 copy.37.q_ref
  117.8 0.8 fusion.13.h_ref
  118.6 64.5 %bring_back.1 = (bf16[8,40,1024]{2,1,0:T(8,128)(2,1)}, f32[1024,1024]{1,0:T(8,128)}, f32[1024,1024]{1,0:T(8,128)}, f32[32,8,128]{2,1,0:T(8,128)}) custom-call(bf16[1280,1024]{1,0:T(8,128)(2,1)} %bitcast.114, f32[1280,1024]{1,0:T(8,128)} %bitcast.120, bf16[1024,1024]{1,0:T(8,128)(2,1)} %bitcast.119, bf16[1280,51]{1,0:T(8,128)(2,1)} %copy.37.q_ref, ...), custom_call_target="tpu_custom_call" | custom-call | tf_op jit(solution)/shard_map/bring_back/pallas_call | solution.py:410
  183.1 0.9 reshape.719
  184.0 0.6 reduce_sum.184
  184.7 2.4 %multiply_reduce_fusion = (f32[1024]{0:T(1024)}, f32[212]{0:T(256)S(1)}, f32[212]{0:T(256)S(1)}, f32[212,1024]{1,0:T(8,128)S(1)}) fusion(bf16[1,212,1024]{2,1,0:T(8,128)(2,1)S(1)} %copy-done.3, f32[212]{0:T(256)S(1)} %add_rsqrt_fusion, f32[212]{0:T(256)S(1)} %broadcast_multiply_fusion.3, f32[1024]{0:T(1024)S(1)} %copy-done.6, ...), kind=kOutput, calls=%fused_computation.20 | convolution fusion | flops 140956512 | bytes 1970320 | tf_op jit(solution)/shard_map/dot_general | solution.py:32
  187.0 16.6 %everyone.1 = f32[8,128]{1,0:T(8,128)} custom-call(f32[8,128]{1,0:T(8,128)} %bitcast.130), custom_call_target="tpu_custom_call" | custom-call | tf_op jit(solution)/shard_map/everyone/pallas_call | solution.py:557
  203.7 1.2 fusion.19
  204.9 4.9 %copy.78 = f32[1,1024,1024]{2,1,0:T(8,128)} copy(f32[1,1024,1024]{2,1,0:T(8,128)} %bitcast.122) | data formatting | bytes 8388608
  209.8 2.0 copy.79
  211.8 0.6 copy.80
  (63 shorter events, 1.5 us)
Async XLA Ops:
  0.6 84.6 %copy-start = (bf16[1,1024,1024]{2,1,0:T(8,128)(2,1)S(1)}, bf16[1,1024,1024]{2,1,0:T(8,128)(2,1)}, u32[]{:S(2)}) copy-start(bf16[1,1024,1024]{2,1,0:T(8,128)(2,1)} %param.15) | copy-start | bytes 6291460
  0.6 11.5 %copy-start.3 = (bf16[1,212,1024]{2,1,0:T(8,128)(2,1)S(1)}, bf16[1,212,1024]{2,1,0:T(8,128)(2,1)}, u32[]{:S(2)}) copy-start(bf16[1,212,1024]{2,1,0:T(8,128)(2,1)} %param.9) | copy-start | bytes 1302532
  112.1 1.9 copy-start.2
  114.0 1.7 copy-start.1
  118.6 66.1 %copy-start.6 = (f32[1024]{0:T(1024)S(1)}, f32[1024]{0:T(1024)}, u32[]{:S(2)}) copy-start(f32[1024]{0:T(1024)} %param.12) | copy-start | bytes 12292
  204.9 4.9 %copy-start.4 = (f32[1024,1024]{1,0:T(8,128)S(1)}, f32[1024,1024]{1,0:T(8,128)}, u32[]{:S(2)}) copy-start(f32[1024,1024]{1,0:T(8,128)} %get-tuple-element.18) | copy-start | bytes 12582916
  209.8 2.0 copy-start.5
